TPU v7x, 32 devices: a whole 2x2x4 slice. The times are simulated.
32 devices in a mesh: pts: 8 (over y, x, core), cam: 4 (over z).
Axes of the slice: x: 2, y: 2, z: 4, core: 2. Of those that a mesh axis runs over, the one named last changes fastest.
Arguments:
- cameras: float32 [9, 4096], P(None, ('pts', 'cam')), may hold values from -0.5 to 2
- increment: float32 [9, 4096], P(None, ('pts', 'cam')), may hold values from -0.3 to 0.3
- points: float32 [3, 524288], P(None, 'pts'), may hold values from -6 to 2
- point_gradient: float32 [3, 524288], P(None, 'pts'), may hold values from -1.8 to 1.8
- point_inverse: float32 [9, 524288], P(None, 'pts'), may hold values from -0.35 to 1.6, as said below
- cam_jacobian: bfloat16 [18, 8388608], P(None, ('pts', 'cam')), may hold values from -3 to 3
- point_jacobian: bfloat16 [6, 8388608], P(None, ('pts', 'cam')), may hold values from -3 to 3
- observed: float32 [2, 8388608], P(None, ('pts', 'cam')), may hold values from -10 to 10
- tile_block: int32 [32768], P(('pts', 'cam')), may hold values from 0 to 31
- tile_points: int32 [32768], P(('pts', 'cam')), may hold values from 0 to 255
- obs_camera: int32 [8388608], P(('pts', 'cam')), may hold values from 0 to 127
- obs_point: int32 [8388608], P(('pts', 'cam')), may hold values from 0 to 255
- accept: int32 [], replicated, may hold values from 0 to 1073741823
Outputs:
- residual: float32 [2, 8388608], P(None, ('pts', 'cam'))
- trial_cost: float32 [], replicated
- accepted_points: float32 [3, 524288], P(None, 'pts')
- accepted_cameras: float32 [9, 4096], P(None, ('pts', 'cam'))
Inputs may be any that keep to these rules, and one draw needn't show every extreme that they name: `tile_block`: the block of 128 cameras that all 256 observations of a tile look at. `tile_points`: the block of 256 points of its point group that all 256 observations of a tile look at. `obs_camera`: an observation's camera within its tile's block. `obs_point`: an observation's point within its tile's point block. `accept`: an odd word accepts the step, an even one keeps the old parameters. `point_inverse`: each 3 x 3 block is symmetric with a dominant positive diagonal.
All inputs are finite; a program needn't handle non-finite values.
Results may differ from a plain program's by a relative error of at most 0.0003.
Values sent between devices are 32-bit elements; how exact they have to be, the bound alone decides.
A program may use at most 192 MiB of HBM per device.

v0:
```python
import functools
import math

import jax
import jax.numpy as jnp
from jax import lax
from jax.experimental import pallas as pl
from jax.experimental.pallas import tpu as pltpu
from jax.sharding import PartitionSpec as P

CB = 128
PB = 256
TILE = 256
LANES = 128
GROUP = 8
PITCH = 9
UNROLL = 16
BLOCKS_PER_STEP = 256
MESH = pl.DeviceIdType.MESH


def lane_take(slab, index):
    return jnp.take_along_axis(slab, index, axis=1, mode="promise_in_bounds")


def row_index(ref, row):
    return jnp.broadcast_to(ref[pl.ds(row, 1), :], (8, LANES))


def couple_kernel(
    tile_block, tile_points, cam_jac, point_jac, obs_cam, obs_point, table, out, total, *scratch
):
    step = pl.program_id(0)
    tiles_per_step = obs_cam.shape[0] // 2
    products, masked = scratch[:UNROLL], scratch[UNROLL:]

    @pl.when(step == 0)
    def _():
        total[...] = jnp.zeros_like(total)
        for buffer in masked:
            buffer[...] = jnp.zeros_like(buffer)

    wide = lax.broadcasted_iota(jnp.int32, (16, LANES), 0).astype(jnp.float32)
    ladders = [(wide + 16.0 * k).astype(jnp.bfloat16) for k in range(8)]
    one = jnp.ones((16, LANES), jnp.bfloat16)
    zero = jnp.zeros((16, LANES), jnp.bfloat16)

    def group(g, prod, mask_rows):
        row = pl.multiple_of(g * GROUP, GROUP)
        tile = step * tiles_per_step + g * (GROUP // 2)
        for s in range(GROUP):
            slab = table.at[tile_block[tile + s // 2]]
            index = row_index(obs_cam, row + s)
            lane = pl.multiple_of((row + s) * LANES, LANES)
            jac = cam_jac[:, pl.ds(lane, LANES)].astype(jnp.float32)
            prod[pl.ds(s, 8, stride=PITCH), :] = jac[0:8] * lane_take(slab[0:8, :], index)
            prod[pl.ds(8 * PITCH + s, 8, stride=PITCH), :] = jac[8:16] * lane_take(slab[8:16, :], index)
            tail = lane_take(slab[16:24, :], index)
            prod[pl.ds(16 * PITCH + s, 2, stride=PITCH), :] = jac[16:18] * tail[0:2]
            pjac = point_jac[:, pl.ds(lane, LANES)].astype(jnp.float32)
            prod[pl.ds(18 * PITCH + s, 6, stride=PITCH), :] = pjac
        rows = [prod[PITCH * m : PITCH * m + 8, :] for m in range(24)]
        first = sum(rows[1:9], rows[0])
        second = sum(rows[10:18], rows[9])
        upper = obs_point[pl.ds(row, GROUP), :] >= LANES
        for n in range(3):
            value = rows[18 + n] * first + rows[21 + n] * second
            mask_rows[PITCH * n : PITCH * n + 8, :] = jnp.where(upper, 0.0, value)
            mask_rows[PITCH * (n + 4) : PITCH * (n + 4) + 8, :] = jnp.where(upper, value, 0.0)
        for t in range(GROUP // 2):
            heads, hots = [], []
            for s in (2 * t, 2 * t + 1):
                value = mask_rows[pl.ds(s, 8, stride=PITCH), :]
                coarse = value.astype(jnp.bfloat16).astype(jnp.float32)
                heads.append(jnp.concatenate([coarse, value - coarse], axis=0).astype(jnp.bfloat16))
                local = (obs_point[pl.ds(row + s, 1), :] & (LANES - 1)).astype(jnp.float32)
                local = jnp.broadcast_to(local, (16, LANES)).astype(jnp.bfloat16)
                hots.append(
                    jnp.concatenate([jnp.where(step_k == local, one, zero) for step_k in ladders], axis=0)
                )
            summed = lax.dot_general(
                jnp.concatenate(heads, axis=1),
                jnp.concatenate(hots, axis=1),
                (((1,), (1,)), ((), ())),
                preferred_element_type=jnp.float32,
            )
            place = pl.ds(pl.multiple_of(tile_points[tile + t] * 8, 8), 8)
            total[place, :] = total[place, :] + (summed[0:8] + summed[8:16])

    def turn(i, carry):
        for u in range(UNROLL):
            group(i * UNROLL + u, products[u], masked[u])
        return carry

    lax.fori_loop(0, obs_cam.shape[0] // (GROUP * UNROLL), turn, 0)

    @pl.when(step == pl.num_programs(0) - 1)
    def _():
        for n in range(3):
            out[n] = total[pl.ds(n, out.shape[1], stride=4), :]


def project_kernel(
    tile_block, tile_points, obs_cam, obs_point, observed, cam_table, trial, residual, cost, point_table, *scratch
):
    step = pl.program_id(0)
    tiles_per_step = obs_cam.shape[0] // 2

    @pl.when(step == 0)
    def _():
        cost[...] = jnp.zeros_like(cost)
        for n in range(3):
            point_table[pl.ds(n, trial.shape[1], stride=4), :] = trial[n]
            point_table[pl.ds(3, trial.shape[1], stride=4), :] = jnp.zeros_like(trial[n])

    def group(g, buf):
        row = pl.multiple_of(g * GROUP, GROUP)
        tile = step * tiles_per_step + g * (GROUP // 2)
        for s in range(GROUP):
            slab = cam_table.at[tile_block[tile + s // 2]]
            index = row_index(obs_cam, row + s)
            buf[pl.ds(s, 8, stride=PITCH), :] = lane_take(slab[0:8, :], index)
            buf[pl.ds(8 * PITCH + s, 8, stride=PITCH), :] = lane_take(slab[8:16, :], index)
            local = row_index(obs_point, row + s) & (LANES - 1)
            place = pl.ds(pl.multiple_of(tile_points[tile + s // 2] * 8, 8), 8)
            buf[pl.ds(16 * PITCH + s, 8, stride=PITCH), :] = lane_take(point_table[place, :], local)
        rows = [buf[PITCH * m : PITCH * m + 8, :] for m in range(24)]
        cam = rows[:15]
        upper = obs_point[pl.ds(row, GROUP), :] >= LANES
        x, y, z = (
            jnp.where(upper, rows[20 + n], rows[16 + n])
            for n in range(3)
        )
        placed = [
            cam[3 * n] * x + cam[3 * n + 1] * y + cam[3 * n + 2] * z + cam[9 + n] for n in range(3)
        ]
        scale = 1.0 / jnp.maximum(-placed[2], 1.0)
        u, v = placed[0] * scale, placed[1] * scale
        q = u * u + v * v
        factor = cam[12] * (1.0 + q * (cam[13] + cam[14] * q))
        at_u = pl.ds(2 * row, GROUP, stride=2)
        at_v = pl.ds(2 * row + 1, GROUP, stride=2)
        ru = factor * u - observed[at_u, :]
        rv = factor * v - observed[at_v, :]
        residual[at_u, :] = ru
        residual[at_v, :] = rv
        return ru * ru + rv * rv

    def turn(i, carry):
        for u in range(UNROLL):
            carry = carry + group(i * UNROLL + u, scratch[u])
        return carry

    cost[...] += lax.fori_loop(
        0, obs_cam.shape[0] // (GROUP * UNROLL), turn, jnp.zeros((8, LANES), jnp.float32)
    )


def camera_rows(trial):
    w = trial[0:3]
    angle = jnp.sqrt(jnp.sum(w * w, axis=0))
    cosine = jnp.cos(angle)
    s1 = jnp.sinc(angle / math.pi)
    s2 = 0.5 * jnp.square(jnp.sinc(angle / (2.0 * math.pi)))
    a, b, c = w[0], w[1], w[2]
    rotation = [
        cosine + s2 * a * a, s2 * a * b - s1 * c, s2 * a * c + s1 * b,
        s2 * a * b + s1 * c, cosine + s2 * b * b, s2 * b * c - s1 * a,
        s2 * a * c - s1 * b, s2 * b * c + s1 * a, cosine + s2 * c * c,
    ]
    return jnp.concatenate([jnp.stack(rotation), trial[3:9]], axis=0)


def greet(axis, size, me):
    barrier = pltpu.get_barrier_semaphore()
    for d in range(1, size):
        pl.semaphore_signal(
            barrier, inc=1, device_id={axis: lax.rem(me + d, size)}, device_id_type=MESH
        )


def send_round(axis, size, me, source, target, send, recv):
    copies = []
    for d in range(1, size):
        peer = lax.rem(me + d, size)
        copies.append(
            pltpu.make_async_remote_copy(
                src_ref=source(peer, d),
                dst_ref=target(peer, d),
                send_sem=send.at[d - 1],
                recv_sem=recv.at[d - 1],
                device_id={axis: peer},
                device_id_type=MESH,
            )
        )
    for copy in copies:
        copy.start()
    return copies


def gather_kernel(n_pts, n_cam, own, out, local_sem, send_cam, recv_cam, send_pts, recv_pts):
    p, c = lax.axis_index("pts"), lax.axis_index("cam")
    greet("pts", n_pts, p)
    greet("cam", n_cam, c)
    pl.semaphore_wait(pltpu.get_barrier_semaphore(), n_pts + n_cam - 2)
    count = own.shape[0]
    mine = out.at[pl.ds((p * n_cam + c) * count, count)]
    local = pltpu.make_async_copy(own, mine, local_sem)
    local.start()
    copies = send_round("cam", n_cam, c, lambda *_: own, lambda *_: mine, send_cam, recv_cam)
    local.wait()
    for copy in copies:
        copy.wait()
    slab = out.at[pl.ds(p * n_cam * count, n_cam * count)]
    for copy in send_round("pts", n_pts, p, lambda *_: slab, lambda *_: slab, send_pts, recv_pts):
        copy.wait()


def solve_kernel(
    n_cam, planes, points, gradient, inverse, out,
    landed, own_points, own_gradient, own_inverse, work, in_sem, send_sum, recv_sum, send_out, recv_out,
):
    c = lax.axis_index("cam")
    rows = planes.shape[1] // n_cam
    span, pitch = rows * LANES, rows + 1
    own_lanes = pl.ds(pl.multiple_of(c * span, span), span)
    loads = [
        pltpu.make_async_copy(source.at[:, own_lanes], target, in_sem.at[i])
        for i, (source, target) in enumerate(
            ((points, own_points), (gradient, own_gradient), (inverse, own_inverse))
        )
    ]
    for load in loads:
        load.start()
    greet("cam", n_cam, c)
    pl.semaphore_wait(pltpu.get_barrier_semaphore(), n_cam - 1)

    def part(peer):
        return pl.ds(pl.multiple_of(peer * rows, 8), rows)

    copies = send_round(
        "cam", n_cam, c,
        lambda peer, d: planes.at[:, part(peer)], lambda peer, d: landed.at[d - 1], send_sum, recv_sum,
    )
    for load in loads:
        load.wait()

    def spread(i, carry):
        for u in range(8):
            k = i * 8 + u
            lanes = pl.ds(pl.multiple_of(k * LANES, LANES), LANES)
            work[pl.ds(k, 3, stride=pitch), :] = own_points[:, lanes]
            work[pl.ds(3 * pitch + k, 3, stride=pitch), :] = own_gradient[:, lanes]
            block = own_inverse[:, lanes]
            work[pl.ds(6 * pitch + k, 8, stride=pitch), :] = block[0:8]
            work[pl.ds(14 * pitch + k, 1), :] = block[8:9]
        return carry

    lax.fori_loop(0, rows // 8, spread, 0)
    for copy in copies:
        copy.wait()

    def solve(i, carry):
        at = pl.multiple_of(i * 8, 8)
        own = pl.multiple_of(c * rows + at, 8)

        def row(m):
            return work[pl.ds(m * pitch + at, 8), :]

        residue = []
        for n in range(3):
            value = planes[n, pl.ds(own, 8), :]
            for d in range(n_cam - 1):
                value = value + landed[d, n, pl.ds(at, 8), :]
            residue.append(row(3 + n) - value)
        for n in range(3):
            move = row(6 + 3 * n) * residue[0] + row(7 + 3 * n) * residue[1] + row(8 + 3 * n) * residue[2]
            out[n, pl.ds(own, 8), :] = row(n) + move
        return carry

    lax.fori_loop(0, rows // 8, solve, 0)
    mine = out.at[:, part(c)]
    for copy in send_round("cam", n_cam, c, lambda *_: mine, lambda *_: mine, send_out, recv_out):
        copy.wait()


def total_kernel(n_pts, n_cam, own, out, cam_slots, pts_slots, send_cam, recv_cam, send_pts, recv_pts):
    p, c = lax.axis_index("pts"), lax.axis_index("cam")
    greet("pts", n_pts, p)
    greet("cam", n_cam, c)
    cam_slots[c] = own[...]
    pl.semaphore_wait(pltpu.get_barrier_semaphore(), n_pts + n_cam - 2)
    slot = cam_slots.at[c]
    for copy in send_round("cam", n_cam, c, lambda *_: own, lambda *_: slot, send_cam, recv_cam):
        copy.wait()
    value = cam_slots[0]
    for i in range(1, n_cam):
        value = value + cam_slots[i]
    pts_slots[p] = value
    slot = pts_slots.at[p]
    for copy in send_round("pts", n_pts, p, lambda *_: slot, lambda *_: slot, send_pts, recv_pts):
        copy.wait()
    value = pts_slots[0]
    for i in range(1, n_pts):
        value = value + pts_slots[i]
    out[...] = value


def on_device(
    cameras, increment, points, point_gradient, point_inverse, cam_jacobian, point_jacobian,
    observed, tile_block, tile_points, obs_camera, obs_point, accept,
):
    own_blocks = cameras.shape[1] // CB
    own = jnp.concatenate([increment, camera_rows(cameras + increment)], axis=0)
    own = own.reshape(24, own_blocks, CB).transpose(1, 0, 2)
    n_pts, n_cam = lax.axis_size("pts"), lax.axis_size("cam")
    vmem = pl.BlockSpec(memory_space=pltpu.VMEM)

    def dma_sems(*counts):
        return [pltpu.SemaphoreType.DMA((count,)) for count in counts]

    def remote(ident):
        return pltpu.CompilerParams(
            collective_id=ident, has_side_effects=True, vmem_limit_bytes=50 * 2**20
        )

    every = pl.pallas_call(
        functools.partial(gather_kernel, n_pts, n_cam),
        in_specs=[vmem],
        out_specs=vmem,
        out_shape=jax.ShapeDtypeStruct((own_blocks * n_pts * n_cam, 24, CB), jnp.float32),
        scratch_shapes=[pltpu.SemaphoreType.DMA]
        + dma_sems(n_cam - 1, n_cam - 1, n_pts - 1, n_pts - 1),
        compiler_params=remote(0),
        name="cameras",
    )(own)
    cam_blocks = every.shape[0]
    steps = every[:, 0:9]
    step_table = jnp.concatenate([steps, steps, jnp.zeros((cam_blocks, 6, CB), jnp.float32)], axis=1)
    cam_table = jnp.concatenate([every[:, 9:24], jnp.zeros((cam_blocks, 1, CB), jnp.float32)], axis=1)

    obs_count = obs_camera.shape[0]
    rows = obs_count // LANES
    per = math.gcd(rows, BLOCKS_PER_STEP)
    grid = (rows // per,)
    point_blocks = points.shape[1] // PB
    oc = obs_camera.reshape(rows, LANES)
    op = obs_point.reshape(rows, LANES)

    def whole(*shape):
        return pl.BlockSpec(shape, lambda i, *_: (0,) * len(shape))

    params = pltpu.CompilerParams(dimension_semantics=("arbitrary",), vmem_limit_bytes=50 * 2**20)
    planes = pl.pallas_call(
        couple_kernel,
        grid_spec=pltpu.PrefetchScalarGridSpec(
            num_scalar_prefetch=2,
            grid=grid,
            in_specs=[
                pl.BlockSpec((18, per * LANES), lambda i, *_: (0, i)),
                pl.BlockSpec((6, per * LANES), lambda i, *_: (0, i)),
                pl.BlockSpec((per, LANES), lambda i, *_: (i, 0)),
                pl.BlockSpec((per, LANES), lambda i, *_: (i, 0)),
                whole(cam_blocks, 24, CB),
            ],
            out_specs=whole(3, 2 * point_blocks, LANES),
            scratch_shapes=[pltpu.VMEM((point_blocks * 8, LANES), jnp.float32)]
            + [pltpu.VMEM((24 * PITCH, LANES), jnp.float32)] * UNROLL
            + [pltpu.VMEM((8 * PITCH, LANES), jnp.float32)] * UNROLL,
        ),
        out_shape=jax.ShapeDtypeStruct((3, 2 * point_blocks, LANES), jnp.float32),
        compiler_params=params,
        name="couple",
    )(tile_block, tile_points, cam_jacobian, point_jacobian, oc, op, step_table)

    own_rows = 2 * point_blocks // n_cam
    hbm = pl.BlockSpec(memory_space=pl.ANY)
    trial = pl.pallas_call(
        functools.partial(solve_kernel, n_cam),
        in_specs=[vmem, hbm, hbm, hbm],
        out_specs=vmem,
        out_shape=jax.ShapeDtypeStruct(planes.shape, jnp.float32),
        scratch_shapes=[
            pltpu.VMEM((n_cam - 1, 3, own_rows, LANES), jnp.float32),
            pltpu.VMEM((3, own_rows * LANES), jnp.float32),
            pltpu.VMEM((3, own_rows * LANES), jnp.float32),
            pltpu.VMEM((9, own_rows * LANES), jnp.float32),
            pltpu.VMEM((15 * (own_rows + 1), LANES), jnp.float32),
        ]
        + dma_sems(3, n_cam - 1, n_cam - 1, n_cam - 1, n_cam - 1),
        compiler_params=remote(1),
        name="solve",
    )(planes, points, point_gradient, point_inverse)

    seen = observed.reshape(2, rows, LANES).transpose(1, 0, 2).reshape(2 * rows, LANES)
    residual, partial = pl.pallas_call(
        project_kernel,
        grid_spec=pltpu.PrefetchScalarGridSpec(
            num_scalar_prefetch=2,
            grid=grid,
            in_specs=[
                pl.BlockSpec((per, LANES), lambda i, *_: (i, 0)),
                pl.BlockSpec((per, LANES), lambda i, *_: (i, 0)),
                pl.BlockSpec((2 * per, LANES), lambda i, *_: (i, 0)),
                whole(cam_blocks, 16, CB),
                whole(3, 2 * point_blocks, LANES),
            ],
            out_specs=[
                pl.BlockSpec((2 * per, LANES), lambda i, *_: (i, 0)),
                whole(8, LANES),
            ],
            scratch_shapes=[pltpu.VMEM((point_blocks * 8, LANES), jnp.float32)]
            + [pltpu.VMEM((24 * PITCH, LANES), jnp.float32)] * UNROLL,
        ),
        out_shape=[
            jax.ShapeDtypeStruct((2 * rows, LANES), jnp.float32),
            jax.ShapeDtypeStruct((8, LANES), jnp.float32),
        ],
        compiler_params=params,
        name="project",
    )(tile_block, tile_points, oc, op, seen, cam_table, trial)
    residual = residual.reshape(rows, 2, LANES).transpose(1, 0, 2).reshape(2, obs_count)
    sums = pl.pallas_call(
        functools.partial(total_kernel, n_pts, n_cam),
        in_specs=[vmem],
        out_specs=vmem,
        out_shape=jax.ShapeDtypeStruct((8, LANES), jnp.float32),
        scratch_shapes=[
            pltpu.VMEM((n_cam, 8, LANES), jnp.float32),
            pltpu.VMEM((n_pts, 8, LANES), jnp.float32),
        ]
        + dma_sems(n_cam - 1, n_cam - 1, n_pts - 1, n_pts - 1),
        compiler_params=remote(2),
        name="total",
    )(partial)
    trial_cost = jnp.sum(sums) / (2.0 * obs_count * n_pts * n_cam)
    odd = jnp.remainder(accept, 2)
    accepted_points = jnp.where(odd == 1, trial.reshape(3, -1), points)
    return residual, trial_cost, accepted_points, cameras + odd.astype(jnp.float32) * increment


def solution(mesh):
    in_specs = (
        P(None, ("pts", "cam")),
        P(None, ("pts", "cam")),
        P(None, "pts"),
        P(None, "pts"),
        P(None, "pts"),
        P(None, ("pts", "cam")),
        P(None, ("pts", "cam")),
        P(None, ("pts", "cam")),
        P(("pts", "cam")),
        P(("pts", "cam")),
        P(("pts", "cam")),
        P(("pts", "cam")),
        P(),
    )
    out_specs = (P(None, ("pts", "cam")), P(), P(None, "pts"), P(None, ("pts", "cam")))
    return jax.shard_map(
        on_device, mesh=mesh, in_specs=in_specs, out_specs=out_specs, check_vma=False
    )
```

profile of v0, /device:TPU:0, one launch (start us, length us, event | category | flops | bytes accessed | tf_op | source)
XLA Modules:
  0.0 120.9 jit_solution(18177318056735010860)
XLA Ops:
  1.3 1.3 %multiply_add_fusion = (f32[9,128]{1,0:T(8,128)}, f32[9,128]{1,0:T(8,128)S(1)}) fusion(f32[9,128]{1,0:T(8,128)} %param.14, f32[9,128]{1,0:T(8,128)} %param.15, f32[]{:T(128)S(6)} %convert_element_type.6), kind=kLoop, calls=%fused_computation.2 | loop fusion | flops 3456 | bytes 18436 | tf_op jit(solution)/shard_map/add | solution.py:439
  2.7 0.1 add_bitcast_fusion
  2.8 0.1 add_bitcast_fusion.2
  2.8 0.7 concatenate.9
  3.6 13.8 %cameras.1 = f32[32,24,128]{2,1,0:T(8,128)S(1)} custom-call(f32[1,24,128]{2,1,0:T(8,128)S(1)} %bitcast.84), custom_call_target="tpu_custom_call" | custom-call | tf_op jit(solution)/shard_map/cameras/pallas_call | solution.py:327
  17.5 0.1 pad.3.clone
  17.5 0.1 maximum_maximum_fusion.table
  17.6 0.0 copy-start
  17.6 1.2 %copy-done = s32[262144]{0:T(1024)S(1)} copy-done((s32[262144]{0:T(1024)S(1)}, s32[262144]{0:T(1024)}, u32[]{:S(2)}) %copy-start) | copy-done | bytes 1048600
  18.9 1.2 %copy-done.2 = s32[262144]{0:T(1024)S(1)} copy-done((s32[262144]{0:T(1024)S(1)}, s32[262144]{0:T(1024)}, u32[]{:S(2)}) %copy-start.2) | copy-done | bytes 1048600
  20.1 0.7 copy-done.6
  20.8 0.7 copy-done.7
  21.5 25.3 %couple.1.planes = f32[3,512,128]{2,1,0:T(8,128)S(1)} custom-call(s32[1024]{0:T(1024)S(1)} %copy-done.6, s32[1024]{0:T(1024)S(1)} %copy-done.7, bf16[18,262144]{1,0:T(8,128)(2,1)} %cam_jac.1, bf16[6,262144]{1,0:T(8,128)(2,1)} %point_jac.1, s32[2048,128]{1,0:T(8,128)S(1)} %bitcast.80, s32[2048,128]{1,0:T(8,128)S(1)} %bitcast.82, ...), custom_call_target="tpu_custom_call" | custom-call | tf_op jit(solution)/shard_map/couple/pallas_call | solution.py:354
  46.7 0.0 copy-done.4
  46.7 0.0 copy-done.5
  46.7 0.0 copy-start.1
  46.8 0.0 copy-start.3
  46.8 35.0 %solve.1.trial = f32[3,512,128]{2,1,0:T(8,128)S(1)} custom-call(f32[3,512,128]{2,1,0:T(8,128)S(1)} %couple.1.planes, f32[3,65536]{1,0:T(4,128)S(1)} %copy-done.4, f32[3,65536]{1,0:T(4,128)S(1)} %copy-done.5, f32[9,65536]{1,0:T(8,128)} %inverse.1), custom_call_target="tpu_custom_call" | custom-call | tf_op jit(solution)/shard_map/solve/pallas_call | solution.py:378
  81.8 0.0 copy-done.1
  81.8 0.0 copy-done.3
  81.8 22.5 %project.1 = (f32[4096,128]{1,0:T(8,128)}, f32[8,128]{1,0:T(8,128)S(1)}) custom-call(s32[1024]{0:T(1024)S(1)} %copy-done.6, s32[1024]{0:T(1024)S(1)} %copy-done.7, s32[2048,128]{1,0:T(8,128)S(1)} %bitcast.81, s32[2048,128]{1,0:T(8,128)S(1)} %bitcast.83, f32[4096,128]{1,0:T(8,128)} %bitcast.85, f32[32,16,128]{2,1,0:T(8,128)S(1)} %concatenate.10.cam_table, ...), custom_call_target="tpu_custom_call" | custom-call | tf_op jit(solution)/shard_map/project/pallas_call | solution.py:396
  104.3 12.6 %total.1 = f32[8,128]{1,0:T(8,128)S(1)} custom-call(f32[8,128]{1,0:T(8,128)S(1)} %get-tuple-element.8.own), custom_call_target="tpu_custom_call" | custom-call | tf_op jit(solution)/shard_map/total/pallas_call | solution.py:423
  116.9 0.6 reduce_sum.19
  118.1 1.6 %bitcast_select_fusion = f32[3,65536]{1,0:T(4,128)} fusion(f32[3,65536]{1,0:T(4,128)S(1)} %copy-done.4, f32[1,3,512,128]{3,2,1,0:T(8,128)S(1)} %bitcast.79, pred[]{:T(512)S(6)} %eq.17), kind=kLoop, calls=%fused_computation | loop fusion | flops 196608 | bytes 2359297 | tf_op jit(solution)/shard_map/jit(_where)/select_n | solution.py:438
  (13 shorter events, 0.2 us)
Async XLA Ops:
  17.6 1.2 %copy-start = (s32[262144]{0:T(1024)S(1)}, s32[262144]{0:T(1024)}, u32[]{:S(2)}) copy-start(s32[262144]{0:T(1024)} %param.24) | copy-start | bytes 3145732
  18.9 1.2 %copy-start.2 = (s32[262144]{0:T(1024)S(1)}, s32[262144]{0:T(1024)}, u32[]{:S(2)}) copy-start(s32[262144]{0:T(1024)} %param.25) | copy-start | bytes 3145732
  20.1 0.7 copy-start.6
  20.8 0.7 copy-start.7
  21.5 25.3 %copy-start.4 = (f32[3,65536]{1,0:T(4,128)S(1)}, f32[3,65536]{1,0:T(4,128)}, u32[]{:S(2)}) copy-start(f32[3,65536]{1,0:T(4,128)} %points.1) | copy-start | bytes 2359300
  21.5 25.3 %copy-start.5 = (f32[3,65536]{1,0:T(4,128)S(1)}, f32[3,65536]{1,0:T(4,128)}, u32[]{:S(2)}) copy-start(f32[3,65536]{1,0:T(4,128)} %gradient.1) | copy-start | bytes 2359300
  46.7 35.1 %copy-start.1 = (s32[262144]{0:T(1024)S(1)}, s32[262144]{0:T(1024)}, u32[]{:S(2)}) copy-start(s32[262144]{0:T(1024)} %param.24) | copy-start | bytes 3145732
  46.8 35.1 %copy-start.3 = (s32[262144]{0:T(1024)S(1)}, s32[262144]{0:T(1024)}, u32[]{:S(2)}) copy-start(s32[262144]{0:T(1024)} %param.25) | copy-start | bytes 3145732
where the time goes:
time: 121 us
  Pallas kernels  109 us (90%)
  local copies, waits for them, and re-layouts  4.73 us (4%)
  other arithmetic  3.83 us (3%)
  between operations  3.23 us (3%)
    pallas_call x1, Pallas kernels, on_device(): pl.pallas_call(functools.partial(solve_kernel, n_cam), in_specs=[vmem, hb...  35 us
    pallas_call x1, Pallas kernels, on_device(): pl.pallas_call(couple_kernel, grid_spec=pltpu.PrefetchScalarGridSpec(num_...  25.3 us
    pallas_call x1, Pallas kernels, on_device(): pl.pallas_call(project_kernel, grid_spec=pltpu.PrefetchScalarGridSpec(num...  22.5 us
    pallas_call x1, Pallas kernels, on_device(): pl.pallas_call(functools.partial(gather_kernel, n_pts, n_cam), in_specs=[...  13.8 us
    pallas_call x1, Pallas kernels, on_device(): pl.pallas_call(functools.partial(total_kernel, n_pts, n_cam), in_specs=[v...  12.6 us
    unnamed x16, local copies, waits for them, and re-layouts  3.84 us

commit v1 on v0

--- a/solution.py
+++ b/solution.py
@@ -15,12 +15,25 @@
 GROUP = 8
 PITCH = 9
 UNROLL = 16
+TILES = 8
+SPREAD = 8
 BLOCKS_PER_STEP = 256
 MESH = pl.DeviceIdType.MESH
 
 
+LANE_GATHER = lax.GatherDimensionNumbers(
+    offset_dims=(),
+    collapsed_slice_dims=(1,),
+    start_index_map=(1,),
+    operand_batching_dims=(0,),
+    start_indices_batching_dims=(0,),
+)
+
+
 def lane_take(slab, index):
-    return jnp.take_along_axis(slab, index, axis=1, mode="promise_in_bounds")
+    return lax.gather(
+        slab, index[:, :, None], LANE_GATHER, (1, 1), mode=lax.GatherScatterMode.PROMISE_IN_BOUNDS
+    )
 
 
 def row_index(ref, row):
@@ -113,62 +126,62 @@
             point_table[pl.ds(n, trial.shape[1], stride=4), :] = trial[n]
             point_table[pl.ds(3, trial.shape[1], stride=4), :] = jnp.zeros_like(trial[n])
 
-    def group(g, buf):
-        row = pl.multiple_of(g * GROUP, GROUP)
-        tile = step * tiles_per_step + g * (GROUP // 2)
-        for s in range(GROUP):
-            slab = cam_table.at[tile_block[tile + s // 2]]
-            index = row_index(obs_cam, row + s)
-            buf[pl.ds(s, 8, stride=PITCH), :] = lane_take(slab[0:8, :], index)
-            buf[pl.ds(8 * PITCH + s, 8, stride=PITCH), :] = lane_take(slab[8:16, :], index)
-            local = row_index(obs_point, row + s) & (LANES - 1)
-            place = pl.ds(pl.multiple_of(tile_points[tile + s // 2] * 8, 8), 8)
-            buf[pl.ds(16 * PITCH + s, 8, stride=PITCH), :] = lane_take(point_table[place, :], local)
-        rows = [buf[PITCH * m : PITCH * m + 8, :] for m in range(24)]
-        cam = rows[:15]
-        upper = obs_point[pl.ds(row, GROUP), :] >= LANES
-        x, y, z = (
-            jnp.where(upper, rows[20 + n], rows[16 + n])
-            for n in range(3)
-        )
-        placed = [
-            cam[3 * n] * x + cam[3 * n + 1] * y + cam[3 * n + 2] * z + cam[9 + n] for n in range(3)
-        ]
-        scale = 1.0 / jnp.maximum(-placed[2], 1.0)
-        u, v = placed[0] * scale, placed[1] * scale
-        q = u * u + v * v
-        factor = cam[12] * (1.0 + q * (cam[13] + cam[14] * q))
-        at_u = pl.ds(2 * row, GROUP, stride=2)
-        at_v = pl.ds(2 * row + 1, GROUP, stride=2)
-        ru = factor * u - observed[at_u, :]
-        rv = factor * v - observed[at_v, :]
-        residual[at_u, :] = ru
-        residual[at_v, :] = rv
-        return ru * ru + rv * rv
+    def group(block, buf):
+        row = pl.multiple_of(block * 2 * TILES, 2 * TILES)
+        tile = step * tiles_per_step + block * TILES
+        for t in range(TILES):
+            slab = cam_table.at[tile_block[tile + t]]
+            buf[pl.ds(t, 8, stride=PITCH), :] = slab[0:8, :]
+            buf[pl.ds(8 * PITCH + t, 2, stride=PITCH), :] = slab[8:10, :]
+            place = pl.ds(pl.multiple_of(tile_points[tile + t] * 8, 8), 8)
+            buf[pl.ds(10 * PITCH + t, 8, stride=PITCH), :] = point_table[place, :]
+        sources = [buf[PITCH * m : PITCH * m + 8, :] for m in range(18)]
+        total = None
+        for h in range(2):
+            at = pl.ds(row + h, TILES, stride=2)
+            index = obs_cam[at, :]
+            head, a, b, c, *shift, focal, k1, k2 = (lane_take(sources[m], index) for m in range(10))
+            point = obs_point[at, :]
+            local = point & (LANES - 1)
+            upper = point >= LANES
+            x, y, z = (
+                jnp.where(upper, lane_take(sources[14 + n], local), lane_take(sources[10 + n], local))
+                for n in range(3)
+            )
+            e, f, g = b * z - c * y, c * x - a * z, a * y - b * x
+            px = x + shift[0] + (head * e + (b * g - c * f))
+            py = y + shift[1] + (head * f + (c * e - a * g))
+            pz = z + shift[2] + (head * g + (a * f - b * e))
+            scale = 1.0 / jnp.maximum(-pz, 1.0)
+            u, v = px * scale, py * scale
+            q = u * u + v * v
+            factor = focal * (1.0 + q * (k1 + k2 * q))
+            at_u = pl.ds(2 * (row + h), TILES, stride=4)
+            at_v = pl.ds(2 * (row + h) + 1, TILES, stride=4)
+            ru = factor * u - observed[at_u, :]
+            rv = factor * v - observed[at_v, :]
+            residual[at_u, :] = ru
+            residual[at_v, :] = rv
+            square = ru * ru + rv * rv
+            total = square if total is None else total + square
+        return total
 
     def turn(i, carry):
-        for u in range(UNROLL):
-            carry = carry + group(i * UNROLL + u, scratch[u])
+        for u in range(SPREAD):
+            carry = carry + group(i * SPREAD + u, scratch[u])
         return carry
 
     cost[...] += lax.fori_loop(
-        0, obs_cam.shape[0] // (GROUP * UNROLL), turn, jnp.zeros((8, LANES), jnp.float32)
+        0, obs_cam.shape[0] // (2 * TILES * SPREAD), turn, jnp.zeros((8, LANES), jnp.float32)
     )
 
 
 def camera_rows(trial):
     w = trial[0:3]
-    angle = jnp.sqrt(jnp.sum(w * w, axis=0))
-    cosine = jnp.cos(angle)
-    s1 = jnp.sinc(angle / math.pi)
-    s2 = 0.5 * jnp.square(jnp.sinc(angle / (2.0 * math.pi)))
-    a, b, c = w[0], w[1], w[2]
-    rotation = [
-        cosine + s2 * a * a, s2 * a * b - s1 * c, s2 * a * c + s1 * b,
-        s2 * a * b + s1 * c, cosine + s2 * b * b, s2 * b * c - s1 * a,
-        s2 * a * c - s1 * b, s2 * b * c + s1 * a, cosine + s2 * c * c,
-    ]
-    return jnp.concatenate([jnp.stack(rotation), trial[3:9]], axis=0)
+    angle = jnp.sqrt(jnp.sum(w * w, axis=0, keepdims=True))
+    head = math.sqrt(2.0) * jnp.cos(0.5 * angle)
+    tail = math.sqrt(0.5) * jnp.sinc(angle / (2.0 * math.pi)) * w
+    return jnp.concatenate([head, tail, trial[3:9]], axis=0)
 
 
 def greet(axis, size, me):
@@ -311,7 +324,9 @@
     observed, tile_block, tile_points, obs_camera, obs_point, accept,
 ):
     own_blocks = cameras.shape[1] // CB
-    own = jnp.concatenate([increment, camera_rows(cameras + increment)], axis=0)
+    own = jnp.concatenate(
+        [increment, camera_rows(cameras + increment), jnp.zeros((5, cameras.shape[1]), jnp.float32)], axis=0
+    )
     own = own.reshape(24, own_blocks, CB).transpose(1, 0, 2)
     n_pts, n_cam = lax.axis_size("pts"), lax.axis_size("cam")
     vmem = pl.BlockSpec(memory_space=pltpu.VMEM)
@@ -337,7 +352,7 @@
     cam_blocks = every.shape[0]
     steps = every[:, 0:9]
     step_table = jnp.concatenate([steps, steps, jnp.zeros((cam_blocks, 6, CB), jnp.float32)], axis=1)
-    cam_table = jnp.concatenate([every[:, 9:24], jnp.zeros((cam_blocks, 1, CB), jnp.float32)], axis=1)
+    cam_table = jnp.concatenate([every[:, 9:19], jnp.zeros((cam_blocks, 6, CB), jnp.float32)], axis=1)
 
     obs_count = obs_camera.shape[0]
     rows = obs_count // LANES
@@ -410,7 +425,7 @@
                 whole(8, LANES),
             ],
             scratch_shapes=[pltpu.VMEM((point_blocks * 8, LANES), jnp.float32)]
-            + [pltpu.VMEM((24 * PITCH, LANES), jnp.float32)] * UNROLL,
+            + [pltpu.VMEM((18 * PITCH, LANES), jnp.float32)] * SPREAD,
         ),
         out_shape=[
             jax.ShapeDtypeStruct((2 * rows, LANES), jnp.float32),

time: 121 us -> 109 us (0.901)
  Pallas kernels: 109 us -> 97.1 us
    pallas_call x1, Pallas kernels: 22.5 us -> 10.6 us  [on_device(): pl.pallas_call(project_kernel, grid_spec=pltpu.PrefetchScalarGridSpec(num...]
where the time goes in v1:
time: 109 us
  Pallas kernels  97.1 us (89%)
  local copies, waits for them, and re-layouts  4.78 us (4%)
  other arithmetic  3.73 us (3%)
  between operations  3.23 us (3%)
    pallas_call x1, Pallas kernels, on_device(): pl.pallas_call(functools.partial(solve_kernel, n_cam), in_specs=[vmem, hb...  35 us
    pallas_call x1, Pallas kernels, on_device(): pl.pallas_call(couple_kernel, grid_spec=pltpu.PrefetchScalarGridSpec(num_...  25.2 us
    pallas_call x1, Pallas kernels, on_device(): pl.pallas_call(functools.partial(gather_kernel, n_pts, n_cam), in_specs=[...  13.9 us
    pallas_call x1, Pallas kernels, on_device(): pl.pallas_call(functools.partial(total_kernel, n_pts, n_cam), in_specs=[v...  12.4 us
    pallas_call x1, Pallas kernels, on_device(): pl.pallas_call(project_kernel, grid_spec=pltpu.PrefetchScalarGridSpec(num...  10.6 us
    unnamed x16, local copies, waits for them, and re-layouts  3.84 us

profile of v1, /device:TPU:0, one launch (start us, length us, event | category | flops | bytes accessed | tf_op | source)
XLA Modules:
  0.0 108.9 jit_solution(10408320248730497723)
XLA Ops:
  1.3 1.3 %multiply_add_fusion = (f32[9,128]{1,0:T(8,128)}, f32[9,128]{1,0:T(8,128)S(1)}) fusion(f32[9,128]{1,0:T(8,128)} %param.13, f32[9,128]{1,0:T(8,128)} %param.14, f32[]{:T(128)S(6)} %convert_element_type.8), kind=kLoop, calls=%fused_computation.2 | loop fusion | flops 3456 | bytes 18436 | tf_op jit(solution)/shard_map/add | solution.py:454
  2.7 0.8 concatenate.9
  3.5 13.9 %cameras.1 = f32[32,24,128]{2,1,0:T(8,128)S(1)} custom-call(f32[1,24,128]{2,1,0:T(8,128)S(1)} %bitcast.23), custom_call_target="tpu_custom_call" | custom-call | tf_op jit(solution)/shard_map/cameras/pallas_call | solution.py:342
  17.4 0.1 pad.3.clone
  17.5 0.1 maximum_maximum_fusion.table
  17.6 0.0 copy-start
  17.6 1.2 %copy-done = s32[262144]{0:T(1024)S(1)} copy-done((s32[262144]{0:T(1024)S(1)}, s32[262144]{0:T(1024)}, u32[]{:S(2)}) %copy-start) | copy-done | bytes 1048600
  18.8 0.0 copy-start.2
  18.8 1.2 %copy-done.2 = s32[262144]{0:T(1024)S(1)} copy-done((s32[262144]{0:T(1024)S(1)}, s32[262144]{0:T(1024)}, u32[]{:S(2)}) %copy-start.2) | copy-done | bytes 1048600
  20.1 0.0 copy-start.6
  20.1 0.7 copy-done.6
  20.7 0.7 copy-done.7
  21.4 25.2 %couple.1.planes = f32[3,512,128]{2,1,0:T(8,128)S(1)} custom-call(s32[1024]{0:T(1024)S(1)} %copy-done.6, s32[1024]{0:T(1024)S(1)} %copy-done.7, bf16[18,262144]{1,0:T(8,128)(2,1)} %cam_jac.1, bf16[6,262144]{1,0:T(8,128)(2,1)} %point_jac.1, s32[2048,128]{1,0:T(8,128)S(1)} %bitcast.19, s32[2048,128]{1,0:T(8,128)S(1)} %bitcast.21, ...), custom_call_target="tpu_custom_call" | custom-call | tf_op jit(solution)/shard_map/couple/pallas_call | solution.py:369
  46.7 0.0 copy-done.4
  46.7 0.0 copy-done.5
  46.7 0.0 copy-start.1
  46.7 0.0 copy-start.3
  46.7 35.0 %solve.1.trial = f32[3,512,128]{2,1,0:T(8,128)S(1)} custom-call(f32[3,512,128]{2,1,0:T(8,128)S(1)} %couple.1.planes, f32[3,65536]{1,0:T(4,128)S(1)} %copy-done.4, f32[3,65536]{1,0:T(4,128)S(1)} %copy-done.5, f32[9,65536]{1,0:T(8,128)} %inverse.1), custom_call_target="tpu_custom_call" | custom-call | tf_op jit(solution)/shard_map/solve/pallas_call | solution.py:393
  81.8 0.0 copy-done.1
  81.8 0.0 copy-done.3
  81.8 10.6 %project.1 = (f32[4096,128]{1,0:T(8,128)}, f32[8,128]{1,0:T(8,128)S(1)}) custom-call(s32[1024]{0:T(1024)S(1)} %copy-done.6, s32[1024]{0:T(1024)S(1)} %copy-done.7, s32[2048,128]{1,0:T(8,128)S(1)} %bitcast.20, s32[2048,128]{1,0:T(8,128)S(1)} %bitcast.22, f32[4096,128]{1,0:T(8,128)} %bitcast.24, f32[32,16,128]{2,1,0:T(8,128)S(1)} %concatenate.10.cam_table, ...), custom_call_target="tpu_custom_call" | custom-call | tf_op jit(solution)/shard_map/project/pallas_call | solution.py:411
  92.4 12.4 %total.1 = f32[8,128]{1,0:T(8,128)S(1)} custom-call(f32[8,128]{1,0:T(8,128)S(1)} %get-tuple-element.7.own), custom_call_target="tpu_custom_call" | custom-call | tf_op jit(solution)/shard_map/total/pallas_call | solution.py:438
  104.9 0.6 reduce_sum.19
  106.1 1.6 %bitcast_select_fusion = f32[3,65536]{1,0:T(4,128)} fusion(f32[3,65536]{1,0:T(4,128)S(1)} %copy-done.4, f32[1,3,512,128]{3,2,1,0:T(8,128)S(1)} %bitcast.18, pred[]{:T(512)S(6)} %eq.40), kind=kLoop, calls=%fused_computation | loop fusion | flops 196608 | bytes 2359297 | tf_op jit(solution)/shard_map/jit(_where)/select_n | solution.py:453
  (12 shorter events, 0.1 us)
Async XLA Ops:
  17.6 1.2 %copy-start = (s32[262144]{0:T(1024)S(1)}, s32[262144]{0:T(1024)}, u32[]{:S(2)}) copy-start(s32[262144]{0:T(1024)} %param.23) | copy-start | bytes 3145732
  18.8 1.2 %copy-start.2 = (s32[262144]{0:T(1024)S(1)}, s32[262144]{0:T(1024)}, u32[]{:S(2)}) copy-start(s32[262144]{0:T(1024)} %param.24) | copy-start | bytes 3145732
  20.1 0.7 copy-start.6
  20.7 0.7 copy-start.7
  21.4 25.2 %copy-start.4 = (f32[3,65536]{1,0:T(4,128)S(1)}, f32[3,65536]{1,0:T(4,128)}, u32[]{:S(2)}) copy-start(f32[3,65536]{1,0:T(4,128)} %points.1) | copy-start | bytes 2359300
  21.4 25.3 %copy-start.5 = (f32[3,65536]{1,0:T(4,128)S(1)}, f32[3,65536]{1,0:T(4,128)}, u32[]{:S(2)}) copy-start(f32[3,65536]{1,0:T(4,128)} %gradient.1) | copy-start | bytes 2359300
  46.7 35.1 %copy-start.1 = (s32[262144]{0:T(1024)S(1)}, s32[262144]{0:T(1024)}, u32[]{:S(2)}) copy-start(s32[262144]{0:T(1024)} %param.23) | copy-start | bytes 3145732
  46.7 35.1 %copy-start.3 = (s32[262144]{0:T(1024)S(1)}, s32[262144]{0:T(1024)}, u32[]{:S(2)}) copy-start(s32[262144]{0:T(1024)} %param.24) | copy-start | bytes 3145732

commit v2 on v1

--- a/solution.py
+++ b/solution.py
@@ -12,9 +12,11 @@
 PB = 256
 TILE = 256
 LANES = 128
-GROUP = 8
 PITCH = 9
-UNROLL = 16
+FINE = 64
+FINE_BITS = 6
+COARSE_ROWS = 32
+PAIRS = 8
 TILES = 8
 SPREAD = 8
 BLOCKS_PER_STEP = 256
@@ -36,81 +38,105 @@
     )
 
 
-def row_index(ref, row):
-    return jnp.broadcast_to(ref[pl.ds(row, 1), :], (8, LANES))
-
-
 def couple_kernel(
-    tile_block, tile_points, cam_jac, point_jac, obs_cam, obs_point, table, out, total, *scratch
+    tile_block, tile_points, cam_jac, point_jac, obs_cam, obs_point, table, out, total, packed, *scratch
 ):
     step = pl.program_id(0)
     tiles_per_step = obs_cam.shape[0] // 2
-    products, masked = scratch[:UNROLL], scratch[UNROLL:]
+    buffers = [scratch[5 * u : 5 * u + 5] for u in range(PAIRS)]
+    blocks = packed.shape[0] // 8
 
     @pl.when(step == 0)
     def _():
         total[...] = jnp.zeros_like(total)
-        for buffer in masked:
-            buffer[...] = jnp.zeros_like(buffer)
-
-    wide = lax.broadcasted_iota(jnp.int32, (16, LANES), 0).astype(jnp.float32)
-    ladders = [(wide + 16.0 * k).astype(jnp.bfloat16) for k in range(8)]
+        for _, _, _, low, high in buffers:
+            low[...] = jnp.zeros_like(low)
+            high[...] = jnp.zeros_like(high)
+
+    wide = lax.broadcasted_iota(jnp.int32, (16, LANES), 0)
+    fine = [(wide + 16 * k).astype(jnp.float32).astype(jnp.bfloat16) for k in range(FINE // 16)]
+    half = (wide >= 8).astype(jnp.float32)
+    coarse = [(half + 2.0 * k).astype(jnp.bfloat16) for k in range(PB // FINE // 2)]
     one = jnp.ones((16, LANES), jnp.bfloat16)
     zero = jnp.zeros((16, LANES), jnp.bfloat16)
 
-    def group(g, prod, mask_rows):
-        row = pl.multiple_of(g * GROUP, GROUP)
-        tile = step * tiles_per_step + g * (GROUP // 2)
-        for s in range(GROUP):
-            slab = table.at[tile_block[tile + s // 2]]
-            index = row_index(obs_cam, row + s)
-            lane = pl.multiple_of((row + s) * LANES, LANES)
-            jac = cam_jac[:, pl.ds(lane, LANES)].astype(jnp.float32)
-            prod[pl.ds(s, 8, stride=PITCH), :] = jac[0:8] * lane_take(slab[0:8, :], index)
-            prod[pl.ds(8 * PITCH + s, 8, stride=PITCH), :] = jac[8:16] * lane_take(slab[8:16, :], index)
-            tail = lane_take(slab[16:24, :], index)
-            prod[pl.ds(16 * PITCH + s, 2, stride=PITCH), :] = jac[16:18] * tail[0:2]
-            pjac = point_jac[:, pl.ds(lane, LANES)].astype(jnp.float32)
-            prod[pl.ds(18 * PITCH + s, 6, stride=PITCH), :] = pjac
-        rows = [prod[PITCH * m : PITCH * m + 8, :] for m in range(24)]
-        first = sum(rows[1:9], rows[0])
-        second = sum(rows[10:18], rows[9])
-        upper = obs_point[pl.ds(row, GROUP), :] >= LANES
-        for n in range(3):
-            value = rows[18 + n] * first + rows[21 + n] * second
-            mask_rows[PITCH * n : PITCH * n + 8, :] = jnp.where(upper, 0.0, value)
-            mask_rows[PITCH * (n + 4) : PITCH * (n + 4) + 8, :] = jnp.where(upper, value, 0.0)
-        for t in range(GROUP // 2):
+    def twice(row):
+        return jnp.broadcast_to(row, (16, LANES)).astype(jnp.bfloat16)
+
+    def group(block, steps, *halves):
+        jacs, sides = halves[:2], halves[2:]
+        row = pl.multiple_of(block * 2 * TILES, 2 * TILES)
+        tile = step * tiles_per_step + block * TILES
+        for t in range(TILES):
+            slab = table.at[tile_block[tile + t]]
+            steps[pl.ds(t, 8, stride=PITCH), :] = slab[0:8, :]
+            steps[pl.ds(8 * PITCH + t, 1), :] = slab[8:9, :]
+            for h in range(2):
+                lane = pl.ds(pl.multiple_of((row + 2 * t + h) * LANES, LANES), LANES)
+                jac = cam_jac[:, lane].astype(jnp.float32)
+                jacs[h][pl.ds(t, 8, stride=PITCH), :] = jac[0:8]
+                jacs[h][pl.ds(8 * PITCH + t, 8, stride=PITCH), :] = jac[8:16]
+                jacs[h][pl.ds(16 * PITCH + t, 2, stride=PITCH), :] = jac[16:18]
+                jacs[h][pl.ds(18 * PITCH + t, 6, stride=PITCH), :] = point_jac[:, lane].astype(jnp.float32)
+        sources = [steps[PITCH * m : PITCH * m + 8, :] for m in range(9)]
+        for h in range(2):
+            at = pl.ds(row + h, TILES, stride=2)
+            index = obs_cam[at, :]
+            moves = [lane_take(source, index) for source in sources]
+            jac = [jacs[h][PITCH * m : PITCH * m + 8, :] for m in range(24)]
+            first = sum((jac[m] * moves[m] for m in range(1, 9)), jac[0] * moves[0])
+            second = sum((jac[9 + m] * moves[m] for m in range(1, 9)), jac[9] * moves[0])
+            side = sides[h]
+            for n in range(3):
+                value = jac[18 + n] * first + jac[21 + n] * second
+                head = value.astype(jnp.bfloat16).astype(jnp.float32)
+                side[PITCH * n : PITCH * n + 8, :] = head
+                side[PITCH * (n + 4) : PITCH * (n + 4) + 8, :] = value - head
+            point = obs_point[at, :]
+            side[PITCH * 8 : PITCH * 8 + 8, :] = (point & (FINE - 1)).astype(jnp.float32)
+            side[PITCH * 9 : PITCH * 9 + 8, :] = (point >> FINE_BITS).astype(jnp.float32)
+        for t in range(TILES):
             heads, hots = [], []
-            for s in (2 * t, 2 * t + 1):
-                value = mask_rows[pl.ds(s, 8, stride=PITCH), :]
-                coarse = value.astype(jnp.bfloat16).astype(jnp.float32)
-                heads.append(jnp.concatenate([coarse, value - coarse], axis=0).astype(jnp.bfloat16))
-                local = (obs_point[pl.ds(row + s, 1), :] & (LANES - 1)).astype(jnp.float32)
-                local = jnp.broadcast_to(local, (16, LANES)).astype(jnp.bfloat16)
-                hots.append(
-                    jnp.concatenate([jnp.where(step_k == local, one, zero) for step_k in ladders], axis=0)
-                )
+            for h in range(2):
+                value = sides[h][pl.ds(t, 8, stride=PITCH), :]
+                value = jnp.concatenate([value, value], axis=0).astype(jnp.bfloat16)
+                low = twice(sides[h][pl.ds(8 * PITCH + t, 1), :])
+                high = twice(sides[h][pl.ds(9 * PITCH + t, 1), :])
+                heads.append(jnp.concatenate([jnp.where(k == high, value, zero) for k in coarse], axis=0))
+                hots.append(jnp.concatenate([jnp.where(k == low, one, zero) for k in fine], axis=0))
             summed = lax.dot_general(
                 jnp.concatenate(heads, axis=1),
                 jnp.concatenate(hots, axis=1),
                 (((1,), (1,)), ((), ())),
                 preferred_element_type=jnp.float32,
             )
-            place = pl.ds(pl.multiple_of(tile_points[tile + t] * 8, 8), 8)
-            total[place, :] = total[place, :] + (summed[0:8] + summed[8:16])
+            place = pl.ds(pl.multiple_of(tile_points[tile + t] * COARSE_ROWS, COARSE_ROWS), COARSE_ROWS)
+            total[place, :] = total[place, :] + summed
 
     def turn(i, carry):
-        for u in range(UNROLL):
-            group(i * UNROLL + u, products[u], masked[u])
+        for u in range(PAIRS):
+            group(i * PAIRS + u, *buffers[u])
         return carry
 
-    lax.fori_loop(0, obs_cam.shape[0] // (GROUP * UNROLL), turn, 0)
+    lax.fori_loop(0, obs_cam.shape[0] // (2 * TILES * PAIRS), turn, 0)
 
     @pl.when(step == pl.num_programs(0) - 1)
     def _():
+        top = lax.broadcasted_iota(jnp.int32, (8, LANES), 0) < 4
+
+        def fold(i, carry):
+            for u in range(8):
+                k = i * 8 + u
+                base = pl.multiple_of(k * COARSE_ROWS, COARSE_ROWS)
+                parts = [total[pl.ds(base + 8 * j, 8), :] for j in range(4)]
+                pair = [jnp.concatenate(parts[2 * j : 2 * j + 2], axis=1) for j in range(2)]
+                pair = [value + pltpu.roll(value, 4, 0) for value in pair]
+                packed[pl.ds(pl.multiple_of(k * 8, 8), 8), :] = jnp.where(top, *pair)
+            return carry
+
+        lax.fori_loop(0, blocks // 8, fold, 0)
         for n in range(3):
-            out[n] = total[pl.ds(n, out.shape[1], stride=4), :]
+            out[n] = packed[pl.ds(n, out.shape[1], stride=4), :]
 
 
 def project_kernel(
@@ -350,8 +376,7 @@
         name="cameras",
     )(own)
     cam_blocks = every.shape[0]
-    steps = every[:, 0:9]
-    step_table = jnp.concatenate([steps, steps, jnp.zeros((cam_blocks, 6, CB), jnp.float32)], axis=1)
+    step_table = jnp.concatenate([every[:, 0:9], jnp.zeros((cam_blocks, 7, CB), jnp.float32)], axis=1)
     cam_table = jnp.concatenate([every[:, 9:19], jnp.zeros((cam_blocks, 6, CB), jnp.float32)], axis=1)
 
     obs_count = obs_camera.shape[0]
@@ -376,12 +401,17 @@
                 pl.BlockSpec((6, per * LANES), lambda i, *_: (0, i)),
                 pl.BlockSpec((per, LANES), lambda i, *_: (i, 0)),
                 pl.BlockSpec((per, LANES), lambda i, *_: (i, 0)),
-                whole(cam_blocks, 24, CB),
+                whole(cam_blocks, 16, CB),
             ],
             out_specs=whole(3, 2 * point_blocks, LANES),
-            scratch_shapes=[pltpu.VMEM((point_blocks * 8, LANES), jnp.float32)]
-            + [pltpu.VMEM((24 * PITCH, LANES), jnp.float32)] * UNROLL
-            + [pltpu.VMEM((8 * PITCH, LANES), jnp.float32)] * UNROLL,
+            scratch_shapes=[
+                pltpu.VMEM((point_blocks * COARSE_ROWS, FINE), jnp.float32),
+                pltpu.VMEM((point_blocks * 8, LANES), jnp.float32),
+            ]
+            + [
+                pltpu.VMEM((count * PITCH, LANES), jnp.float32) for count in (9, 24, 24, 10, 10)
+            ]
+            * PAIRS,
         ),
         out_shape=jax.ShapeDtypeStruct((3, 2 * point_blocks, LANES), jnp.float32),
         compiler_params=params,

time: 109 us -> 106 us (0.972)
  Pallas kernels: 97.1 us -> 93.1 us
    pallas_call x1, Pallas kernels: 25.2 us -> 21.1 us  [on_device(): pl.pallas_call(couple_kernel, grid_spec=pltpu.PrefetchScalarGridSpec(num_...]
where the time goes in v2:
time: 106 us; the launch traced here: 105 us
  Pallas kernels  93.1 us (88%)
  local copies, waits for them, and re-layouts  4.69 us (4%)
  other arithmetic  4.38 us (4%)
  between operations  3.22 us (3%)
    pallas_call x1, Pallas kernels, on_device(): pl.pallas_call(functools.partial(solve_kernel, n_cam), in_specs=[vmem, hb...  35 us
    pallas_call x1, Pallas kernels, on_device(): pl.pallas_call(couple_kernel, grid_spec=pltpu.PrefetchScalarGridSpec(num_...  21.1 us
    pallas_call x1, Pallas kernels, on_device(): pl.pallas_call(functools.partial(gather_kernel, n_pts, n_cam), in_specs=[...  13.9 us
    pallas_call x1, Pallas kernels, on_device(): pl.pallas_call(functools.partial(total_kernel, n_pts, n_cam), in_specs=[v...  12.5 us
    pallas_call x1, Pallas kernels, on_device(): pl.pallas_call(project_kernel, grid_spec=pltpu.PrefetchScalarGridSpec(num...  10.6 us
    unnamed x16, local copies, waits for them, and re-layouts  3.84 us

profile of v2, /device:TPU:0, one launch (start us, length us, event | category | flops | bytes accessed | tf_op | source)
XLA Modules:
  0.0 105.4 jit_solution(15763193341231027632)
XLA Ops:
  1.3 1.3 %multiply_add_fusion = (f32[9,128]{1,0:T(8,128)}, f32[9,128]{1,0:T(8,128)S(1)}) fusion(f32[9,128]{1,0:T(8,128)} %param.13, f32[9,128]{1,0:T(8,128)} %param.14, f32[]{:T(128)S(6)} %convert_element_type.8), kind=kLoop, calls=%fused_computation.2 | loop fusion | flops 3456 | bytes 18436 | tf_op jit(solution)/shard_map/add | solution.py:484
  2.7 0.8 concatenate.9
  3.5 13.9 %cameras.1 = f32[32,24,128]{2,1,0:T(8,128)S(1)} custom-call(f32[1,24,128]{2,1,0:T(8,128)S(1)} %bitcast.23), custom_call_target="tpu_custom_call" | custom-call | tf_op jit(solution)/shard_map/cameras/pallas_call | solution.py:368
  17.4 0.7 slice_select_fusion.table
  18.1 0.0 copy-start
  18.1 1.2 %copy-done = s32[262144]{0:T(1024)S(1)} copy-done((s32[262144]{0:T(1024)S(1)}, s32[262144]{0:T(1024)}, u32[]{:S(2)}) %copy-start) | copy-done | bytes 1048600
  19.4 0.0 copy-start.2
  19.4 1.2 %copy-done.2 = s32[262144]{0:T(1024)S(1)} copy-done((s32[262144]{0:T(1024)S(1)}, s32[262144]{0:T(1024)}, u32[]{:S(2)}) %copy-start.2) | copy-done | bytes 1048600
  20.6 0.0 copy-start.6
  20.6 0.7 copy-done.6
  21.3 0.0 copy-start.7
  21.3 0.7 copy-done.7
  22.0 21.1 %couple.1.planes = f32[3,512,128]{2,1,0:T(8,128)S(1)} custom-call(s32[1024]{0:T(1024)S(1)} %copy-done.6, s32[1024]{0:T(1024)S(1)} %copy-done.7, bf16[18,262144]{1,0:T(8,128)(2,1)} %cam_jac.1, bf16[6,262144]{1,0:T(8,128)(2,1)} %point_jac.1, s32[2048,128]{1,0:T(8,128)S(1)} %bitcast.19, s32[2048,128]{1,0:T(8,128)S(1)} %bitcast.21, ...), custom_call_target="tpu_custom_call" | custom-call | tf_op jit(solution)/shard_map/couple/pallas_call | solution.py:394
  43.1 0.0 copy-done.4
  43.1 0.0 copy-done.5
  43.1 0.0 copy-start.1
  43.1 0.0 copy-start.3
  43.1 35.0 %solve.1.trial = f32[3,512,128]{2,1,0:T(8,128)S(1)} custom-call(f32[3,512,128]{2,1,0:T(8,128)S(1)} %couple.1.planes, f32[3,65536]{1,0:T(4,128)S(1)} %copy-done.4, f32[3,65536]{1,0:T(4,128)S(1)} %copy-done.5, f32[9,65536]{1,0:T(8,128)} %inverse.1), custom_call_target="tpu_custom_call" | custom-call | tf_op jit(solution)/shard_map/solve/pallas_call | solution.py:423
  78.2 0.0 copy-done.1
  78.2 0.0 copy-done.3
  78.2 10.6 %project.1 = (f32[4096,128]{1,0:T(8,128)}, f32[8,128]{1,0:T(8,128)S(1)}) custom-call(s32[1024]{0:T(1024)S(1)} %copy-done.6, s32[1024]{0:T(1024)S(1)} %copy-done.7, s32[2048,128]{1,0:T(8,128)S(1)} %bitcast.20, s32[2048,128]{1,0:T(8,128)S(1)} %bitcast.22, f32[4096,128]{1,0:T(8,128)} %bitcast.24, f32[32,16,128]{2,1,0:T(8,128)S(1)} %concatenate.10.cam_table, ...), custom_call_target="tpu_custom_call" | custom-call | tf_op jit(solution)/shard_map/project/pallas_call | solution.py:441
  88.8 12.5 %total.1 = f32[8,128]{1,0:T(8,128)S(1)} custom-call(f32[8,128]{1,0:T(8,128)S(1)} %get-tuple-element.7.own), custom_call_target="tpu_custom_call" | custom-call | tf_op jit(solution)/shard_map/total/pallas_call | solution.py:468
  101.4 0.6 reduce_sum.19
  102.6 1.6 %bitcast_select_fusion = f32[3,65536]{1,0:T(4,128)} fusion(f32[3,65536]{1,0:T(4,128)S(1)} %copy-done.4, f32[1,3,512,128]{3,2,1,0:T(8,128)S(1)} %bitcast.18, pred[]{:T(512)S(6)} %eq.40), kind=kLoop, calls=%fused_computation | loop fusion | flops 196608 | bytes 2359297 | tf_op jit(solution)/shard_map/jit(_where)/select_n | solution.py:483
  (9 shorter events, 0.1 us)
Async XLA Ops:
  18.1 1.2 %copy-start = (s32[262144]{0:T(1024)S(1)}, s32[262144]{0:T(1024)}, u32[]{:S(2)}) copy-start(s32[262144]{0:T(1024)} %param.23) | copy-start | bytes 3145732
  19.4 1.2 %copy-start.2 = (s32[262144]{0:T(1024)S(1)}, s32[262144]{0:T(1024)}, u32[]{:S(2)}) copy-start(s32[262144]{0:T(1024)} %param.24) | copy-start | bytes 3145732
  20.6 0.7 copy-start.6
  21.3 0.7 copy-start.7
  22.0 21.1 %copy-start.4 = (f32[3,65536]{1,0:T(4,128)S(1)}, f32[3,65536]{1,0:T(4,128)}, u32[]{:S(2)}) copy-start(f32[3,65536]{1,0:T(4,128)} %points.1) | copy-start | bytes 2359300
  22.0 21.1 %copy-start.5 = (f32[3,65536]{1,0:T(4,128)S(1)}, f32[3,65536]{1,0:T(4,128)}, u32[]{:S(2)}) copy-start(f32[3,65536]{1,0:T(4,128)} %gradient.1) | copy-start | bytes 2359300
  43.1 35.1 %copy-start.1 = (s32[262144]{0:T(1024)S(1)}, s32[262144]{0:T(1024)}, u32[]{:S(2)}) copy-start(s32[262144]{0:T(1024)} %param.23) | copy-start | bytes 3145732
  43.1 35.1 %copy-start.3 = (s32[262144]{0:T(1024)S(1)}, s32[262144]{0:T(1024)}, u32[]{:S(2)}) copy-start(s32[262144]{0:T(1024)} %param.24) | copy-start | bytes 3145732

commit v3 on v2

--- a/solution.py
+++ b/solution.py
@@ -19,6 +19,8 @@
 PAIRS = 8
 TILES = 8
 SPREAD = 8
+CHUNKS = 16
+LAG = 4
 BLOCKS_PER_STEP = 256
 MESH = pl.DeviceIdType.MESH
 
@@ -260,67 +262,158 @@
     landed, own_points, own_gradient, own_inverse, work, in_sem, send_sum, recv_sum, send_out, recv_out,
 ):
     c = lax.axis_index("cam")
-    rows = planes.shape[1] // n_cam
+    last = n_cam - 1
+    chunks = landed.shape[1]
+    rows = planes.shape[1] // 2
+    count = rows // chunks
     span, pitch = rows * LANES, rows + 1
-    own_lanes = pl.ds(pl.multiple_of(c * span, span), span)
+    low_end, high_end = c == 0, c == last
+    at_end = jnp.logical_or(low_end, high_end)
+    own_base = jnp.where(low_end, 0, rows)
     loads = [
-        pltpu.make_async_copy(source.at[:, own_lanes], target, in_sem.at[i])
+        pltpu.make_async_copy(
+            source.at[:, pl.ds(pl.multiple_of(own_base * LANES, LANES), span)], target, in_sem.at[i]
+        )
         for i, (source, target) in enumerate(
             ((points, own_points), (gradient, own_gradient), (inverse, own_inverse))
         )
     ]
-    for load in loads:
-        load.start()
-    greet("cam", n_cam, c)
-    pl.semaphore_wait(pltpu.get_barrier_semaphore(), n_cam - 1)
-
-    def part(peer):
-        return pl.ds(pl.multiple_of(peer * rows, 8), rows)
-
-    copies = send_round(
-        "cam", n_cam, c,
-        lambda peer, d: planes.at[:, part(peer)], lambda peer, d: landed.at[d - 1], send_sum, recv_sum,
-    )
-    for load in loads:
-        load.wait()
-
-    def spread(i, carry):
-        for u in range(8):
-            k = i * 8 + u
-            lanes = pl.ds(pl.multiple_of(k * LANES, LANES), LANES)
-            work[pl.ds(k, 3, stride=pitch), :] = own_points[:, lanes]
-            work[pl.ds(3 * pitch + k, 3, stride=pitch), :] = own_gradient[:, lanes]
-            block = own_inverse[:, lanes]
-            work[pl.ds(6 * pitch + k, 8, stride=pitch), :] = block[0:8]
-            work[pl.ds(14 * pitch + k, 1), :] = block[8:9]
-        return carry
-
-    lax.fori_loop(0, rows // 8, spread, 0)
-    for copy in copies:
-        copy.wait()
-
-    def solve(i, carry):
-        at = pl.multiple_of(i * 8, 8)
-        own = pl.multiple_of(c * rows + at, 8)
-
+
+    @pl.when(at_end)
+    def _():
+        for load in loads:
+            load.start()
+
+    barrier = pltpu.get_barrier_semaphore()
+
+    def peer(step):
+        return lax.rem(c + step + n_cam, n_cam)
+
+    @pl.when(c > 0)
+    def _():
+        pl.semaphore_signal(barrier, inc=1, device_id={"cam": peer(-1)}, device_id_type=MESH)
+
+    @pl.when(c < last)
+    def _():
+        pl.semaphore_signal(barrier, inc=1, device_id={"cam": peer(1)}, device_id_type=MESH)
+
+    pl.semaphore_wait(barrier, jnp.where(at_end, 1, 2))
+
+    def place(way, k):
+        base = rows if way == 0 else 0
+        return pl.ds(pl.multiple_of(base + k * count, 8), count)
+
+    def toward(way):
+        return peer(1) if way == 0 else peer(-1)
+
+    def sum_copy(way, k, source):
+        return pltpu.make_async_remote_copy(
+            src_ref=source,
+            dst_ref=landed.at[way, k],
+            send_sem=send_sum.at[way, k],
+            recv_sem=recv_sum.at[way, k],
+            device_id={"cam": toward(way)},
+            device_id_type=MESH,
+        )
+
+    def out_copy(way, k):
+        part = out.at[:, place(way, k)]
+        return pltpu.make_async_remote_copy(
+            src_ref=part,
+            dst_ref=part,
+            send_sem=send_out.at[way, k],
+            recv_sem=recv_out.at[way, k],
+            device_id={"cam": toward(1 - way)},
+            device_id_type=MESH,
+        )
+
+    for way, first in ((0, low_end), (1, high_end)):
+
+        @pl.when(first)
+        def _(way=way):
+            def begin(k, carry):
+                sum_copy(way, k, planes.at[:, place(way, k)]).start()
+                return carry
+
+            lax.fori_loop(0, chunks, begin, 0)
+
+    @pl.when(at_end)
+    def _():
+        for load in loads:
+            load.wait()
+
+        def spread(i, carry):
+            for u in range(8):
+                k = i * 8 + u
+                lanes = pl.ds(pl.multiple_of(k * LANES, LANES), LANES)
+                work[pl.ds(k, 3, stride=pitch), :] = own_points[:, lanes]
+                work[pl.ds(3 * pitch + k, 3, stride=pitch), :] = own_gradient[:, lanes]
+                block = own_inverse[:, lanes]
+                work[pl.ds(6 * pitch + k, 8, stride=pitch), :] = block[0:8]
+                work[pl.ds(14 * pitch + k, 1), :] = block[8:9]
+            return carry
+
+        lax.fori_loop(0, rows // 8, spread, 0)
+
+    def solved(way, k):
         def row(m):
-            return work[pl.ds(m * pitch + at, 8), :]
-
-        residue = []
-        for n in range(3):
-            value = planes[n, pl.ds(own, 8), :]
-            for d in range(n_cam - 1):
-                value = value + landed[d, n, pl.ds(at, 8), :]
-            residue.append(row(3 + n) - value)
+            return work[pl.ds(m * pitch + k * count, count), :]
+
+        total = landed[way, k] + planes[:, place(way, k), :]
+        residue = [row(3 + n) - total[n] for n in range(3)]
         for n in range(3):
             move = row(6 + 3 * n) * residue[0] + row(7 + 3 * n) * residue[1] + row(8 + 3 * n) * residue[2]
-            out[n, pl.ds(own, 8), :] = row(n) + move
+            out[n, place(way, k), :] = row(n) + move
+
+    def turn(s, carry):
+        for way, hops in ((0, c), (1, last - c)):
+            k = s - LAG * hops
+            live = jnp.logical_and(hops > 0, jnp.logical_and(k >= 0, k < chunks))
+
+            @pl.when(live)
+            def _(way=way, k=k, hops=hops):
+                sum_copy(way, k, landed.at[way, k]).wait_recv()
+
+                @pl.when(hops < last)
+                def _():
+                    landed[way, k] = landed[way, k] + planes[:, place(way, k), :]
+                    sum_copy(way, k, landed.at[way, k]).start()
+
+                @pl.when(hops == last)
+                def _():
+                    solved(way, k)
+                    out_copy(way, k).start()
+
+        for way, hops in ((0, last - c), (1, c)):
+            k = s - LAG * (last + hops)
+            live = jnp.logical_and(hops > 0, jnp.logical_and(k >= 0, k < chunks))
+
+            @pl.when(live)
+            def _(way=way, k=k, hops=hops):
+                out_copy(way, k).wait_recv()
+
+                @pl.when(hops < last)
+                def _():
+                    out_copy(way, k).start()
+
         return carry
 
-    lax.fori_loop(0, rows // 8, solve, 0)
-    mine = out.at[:, part(c)]
-    for copy in send_round("cam", n_cam, c, lambda *_: mine, lambda *_: mine, send_out, recv_out):
-        copy.wait()
+    lax.fori_loop(0, chunks + 2 * LAG * last, turn, 0)
+
+    def finish(k, carry):
+        for way, first, end in ((0, low_end, high_end), (1, high_end, low_end)):
+
+            @pl.when(jnp.logical_not(end))
+            def _(way=way):
+                sum_copy(way, k, landed.at[way, k]).wait_send()
+
+            @pl.when(jnp.logical_not(first))
+            def _(way=way):
+                out_copy(way, k).wait_send()
+
+        return carry
+
+    lax.fori_loop(0, chunks, finish, 0)
 
 
 def total_kernel(n_pts, n_cam, own, out, cam_slots, pts_slots, send_cam, recv_cam, send_pts, recv_pts):
@@ -418,7 +511,8 @@
         name="couple",
     )(tile_block, tile_points, cam_jacobian, point_jacobian, oc, op, step_table)
 
-    own_rows = 2 * point_blocks // n_cam
+    own_rows = point_blocks
+    chunks = math.gcd(own_rows // 8, CHUNKS)
     hbm = pl.BlockSpec(memory_space=pl.ANY)
     trial = pl.pallas_call(
         functools.partial(solve_kernel, n_cam),
@@ -426,13 +520,14 @@
         out_specs=vmem,
         out_shape=jax.ShapeDtypeStruct(planes.shape, jnp.float32),
         scratch_shapes=[
-            pltpu.VMEM((n_cam - 1, 3, own_rows, LANES), jnp.float32),
+            pltpu.VMEM((2, chunks, 3, own_rows // chunks, LANES), jnp.float32),
             pltpu.VMEM((3, own_rows * LANES), jnp.float32),
             pltpu.VMEM((3, own_rows * LANES), jnp.float32),
             pltpu.VMEM((9, own_rows * LANES), jnp.float32),
             pltpu.VMEM((15 * (own_rows + 1), LANES), jnp.float32),
+            pltpu.SemaphoreType.DMA((3,)),
         ]
-        + dma_sems(3, n_cam - 1, n_cam - 1, n_cam - 1, n_cam - 1),
+        + [pltpu.SemaphoreType.DMA((2, chunks))] * 4,
         compiler_params=remote(1),
         name="solve",
     )(planes, points, point_gradient, point_inverse)

time: 106 us -> 98.4 us (0.928)
  Pallas kernels: 93.1 us -> 85.6 us
    pallas_call x1, Pallas kernels: 35 us -> 30.7 us  [on_device(): pl.pallas_call(functools.partial(solve_kernel, n_cam), in_specs=[vmem, hb...]
    pallas_call x1, Pallas kernels: 12.5 us -> 9.38 us  [on_device(): pl.pallas_call(functools.partial(total_kernel, n_pts, n_cam), in_specs=[v...]
where the time goes in v3:
time: 98.4 us; the launch traced here: 97.9 us
  Pallas kernels  85.6 us (87%)
  local copies, waits for them, and re-layouts  4.69 us (5%)
  other arithmetic  4.38 us (4%)
  between operations  3.22 us (3%)
    pallas_call x1, Pallas kernels, on_device(): pl.pallas_call(functools.partial(solve_kernel, n_cam), in_specs=[vmem, hb...  30.7 us
    pallas_call x1, Pallas kernels, on_device(): pl.pallas_call(couple_kernel, grid_spec=pltpu.PrefetchScalarGridSpec(num_...  21.1 us
    pallas_call x1, Pallas kernels, on_device(): pl.pallas_call(functools.partial(gather_kernel, n_pts, n_cam), in_specs=[...  13.9 us
    pallas_call x1, Pallas kernels, on_device(): pl.pallas_call(project_kernel, grid_spec=pltpu.PrefetchScalarGridSpec(num...  10.6 us
    pallas_call x1, Pallas kernels, on_device(): pl.pallas_call(functools.partial(total_kernel, n_pts, n_cam), in_specs=[v...  9.38 us
    unnamed x16, local copies, waits for them, and re-layouts  3.84 us

profile of v3, /device:TPU:0, one launch (start us, length us, event | category | flops | bytes accessed | tf_op | source)
XLA Modules:
  0.0 97.9 jit_solution(4519684886252026926)
XLA Ops:
  1.3 1.3 %multiply_add_fusion = (f32[9,128]{1,0:T(8,128)}, f32[9,128]{1,0:T(8,128)S(1)}) fusion(f32[9,128]{1,0:T(8,128)} %param.13, f32[9,128]{1,0:T(8,128)} %param.14, f32[]{:T(128)S(6)} %convert_element_type.8), kind=kLoop, calls=%fused_computation.2 | loop fusion | flops 3456 | bytes 18436 | tf_op jit(solution)/shard_map/add | solution.py:579
  2.7 0.8 concatenate.9
  3.5 13.9 %cameras.1 = f32[32,24,128]{2,1,0:T(8,128)S(1)} custom-call(f32[1,24,128]{2,1,0:T(8,128)S(1)} %bitcast.23), custom_call_target="tpu_custom_call" | custom-call | tf_op jit(solution)/shard_map/cameras/pallas_call | solution.py:461
  17.4 0.7 slice_select_fusion.table
  18.1 0.0 copy-start
  18.1 1.2 %copy-done = s32[262144]{0:T(1024)S(1)} copy-done((s32[262144]{0:T(1024)S(1)}, s32[262144]{0:T(1024)}, u32[]{:S(2)}) %copy-start) | copy-done | bytes 1048600
  19.4 0.0 copy-start.2
  19.4 1.2 %copy-done.2 = s32[262144]{0:T(1024)S(1)} copy-done((s32[262144]{0:T(1024)S(1)}, s32[262144]{0:T(1024)}, u32[]{:S(2)}) %copy-start.2) | copy-done | bytes 1048600
  20.6 0.0 copy-start.6
  20.6 0.7 copy-done.6
  21.3 0.0 copy-start.7
  21.3 0.7 copy-done.7
  22.0 21.1 %couple.1.planes = f32[3,512,128]{2,1,0:T(8,128)S(1)} custom-call(s32[1024]{0:T(1024)S(1)} %copy-done.6, s32[1024]{0:T(1024)S(1)} %copy-done.7, bf16[18,262144]{1,0:T(8,128)(2,1)} %cam_jac.1, bf16[6,262144]{1,0:T(8,128)(2,1)} %point_jac.1, s32[2048,128]{1,0:T(8,128)S(1)} %bitcast.19, s32[2048,128]{1,0:T(8,128)S(1)} %bitcast.21, ...), custom_call_target="tpu_custom_call" | custom-call | tf_op jit(solution)/shard_map/couple/pallas_call | solution.py:487
  43.1 0.0 copy-done.4
  43.1 0.0 copy-done.5
  43.1 0.0 copy-start.1
  43.1 0.0 copy-start.3
  43.1 30.7 %solve.1.trial = f32[3,512,128]{2,1,0:T(8,128)S(1)} custom-call(f32[3,512,128]{2,1,0:T(8,128)S(1)} %couple.1.planes, f32[3,65536]{1,0:T(4,128)S(1)} %copy-done.4, f32[3,65536]{1,0:T(4,128)S(1)} %copy-done.5, f32[9,65536]{1,0:T(8,128)} %inverse.1), custom_call_target="tpu_custom_call" | custom-call | tf_op jit(solution)/shard_map/solve/pallas_call | solution.py:517
  73.8 0.0 copy-done.1
  73.8 0.0 copy-done.3
  73.9 10.6 %project.1 = (f32[4096,128]{1,0:T(8,128)}, f32[8,128]{1,0:T(8,128)S(1)}) custom-call(s32[1024]{0:T(1024)S(1)} %copy-done.6, s32[1024]{0:T(1024)S(1)} %copy-done.7, s32[2048,128]{1,0:T(8,128)S(1)} %bitcast.20, s32[2048,128]{1,0:T(8,128)S(1)} %bitcast.22, f32[4096,128]{1,0:T(8,128)} %bitcast.24, f32[32,16,128]{2,1,0:T(8,128)S(1)} %concatenate.10.cam_table, ...), custom_call_target="tpu_custom_call" | custom-call | tf_op jit(solution)/shard_map/project/pallas_call | solution.py:536
  84.5 9.4 %total.1 = f32[8,128]{1,0:T(8,128)S(1)} custom-call(f32[8,128]{1,0:T(8,128)S(1)} %get-tuple-element.7.own), custom_call_target="tpu_custom_call" | custom-call | tf_op jit(solution)/shard_map/total/pallas_call | solution.py:563
  93.9 0.6 reduce_sum.19
  95.1 1.6 %bitcast_select_fusion = f32[3,65536]{1,0:T(4,128)} fusion(f32[3,65536]{1,0:T(4,128)S(1)} %copy-done.4, f32[1,3,512,128]{3,2,1,0:T(8,128)S(1)} %bitcast.18, pred[]{:T(512)S(6)} %eq.40), kind=kLoop, calls=%fused_computation | loop fusion | flops 196608 | bytes 2359297 | tf_op jit(solution)/shard_map/jit(_where)/select_n | solution.py:578
  (9 shorter events, 0.1 us)
Async XLA Ops:
  18.1 1.2 %copy-start = (s32[262144]{0:T(1024)S(1)}, s32[262144]{0:T(1024)}, u32[]{:S(2)}) copy-start(s32[262144]{0:T(1024)} %param.23) | copy-start | bytes 3145732
  19.4 1.2 %copy-start.2 = (s32[262144]{0:T(1024)S(1)}, s32[262144]{0:T(1024)}, u32[]{:S(2)}) copy-start(s32[262144]{0:T(1024)} %param.24) | copy-start | bytes 3145732
  20.6 0.7 copy-start.6
  21.3 0.7 copy-start.7
  22.0 21.1 %copy-start.4 = (f32[3,65536]{1,0:T(4,128)S(1)}, f32[3,65536]{1,0:T(4,128)}, u32[]{:S(2)}) copy-start(f32[3,65536]{1,0:T(4,128)} %points.1) | copy-start | bytes 2359300
  22.0 21.1 %copy-start.5 = (f32[3,65536]{1,0:T(4,128)S(1)}, f32[3,65536]{1,0:T(4,128)}, u32[]{:S(2)}) copy-start(f32[3,65536]{1,0:T(4,128)} %gradient.1) | copy-start | bytes 2359300
  43.1 30.8 %copy-start.1 = (s32[262144]{0:T(1024)S(1)}, s32[262144]{0:T(1024)}, u32[]{:S(2)}) copy-start(s32[262144]{0:T(1024)} %param.23) | copy-start | bytes 3145732
  43.1 30.8 %copy-start.3 = (s32[262144]{0:T(1024)S(1)}, s32[262144]{0:T(1024)}, u32[]{:S(2)}) copy-start(s32[262144]{0:T(1024)} %param.24) | copy-start | bytes 3145732

commit v4 on v3

--- a/solution.py
+++ b/solution.py
@@ -20,7 +20,7 @@
 TILES = 8
 SPREAD = 8
 CHUNKS = 16
-LAG = 4
+LAG = 5
 BLOCKS_PER_STEP = 256
 MESH = pl.DeviceIdType.MESH
 
@@ -141,69 +141,6 @@
             out[n] = packed[pl.ds(n, out.shape[1], stride=4), :]
 
 
-def project_kernel(
-    tile_block, tile_points, obs_cam, obs_point, observed, cam_table, trial, residual, cost, point_table, *scratch
-):
-    step = pl.program_id(0)
-    tiles_per_step = obs_cam.shape[0] // 2
-
-    @pl.when(step == 0)
-    def _():
-        cost[...] = jnp.zeros_like(cost)
-        for n in range(3):
-            point_table[pl.ds(n, trial.shape[1], stride=4), :] = trial[n]
-            point_table[pl.ds(3, trial.shape[1], stride=4), :] = jnp.zeros_like(trial[n])
-
-    def group(block, buf):
-        row = pl.multiple_of(block * 2 * TILES, 2 * TILES)
-        tile = step * tiles_per_step + block * TILES
-        for t in range(TILES):
-            slab = cam_table.at[tile_block[tile + t]]
-            buf[pl.ds(t, 8, stride=PITCH), :] = slab[0:8, :]
-            buf[pl.ds(8 * PITCH + t, 2, stride=PITCH), :] = slab[8:10, :]
-            place = pl.ds(pl.multiple_of(tile_points[tile + t] * 8, 8), 8)
-            buf[pl.ds(10 * PITCH + t, 8, stride=PITCH), :] = point_table[place, :]
-        sources = [buf[PITCH * m : PITCH * m + 8, :] for m in range(18)]
-        total = None
-        for h in range(2):
-            at = pl.ds(row + h, TILES, stride=2)
-            index = obs_cam[at, :]
-            head, a, b, c, *shift, focal, k1, k2 = (lane_take(sources[m], index) for m in range(10))
-            point = obs_point[at, :]
-            local = point & (LANES - 1)
-            upper = point >= LANES
-            x, y, z = (
-                jnp.where(upper, lane_take(sources[14 + n], local), lane_take(sources[10 + n], local))
-                for n in range(3)
-            )
-            e, f, g = b * z - c * y, c * x - a * z, a * y - b * x
-            px = x + shift[0] + (head * e + (b * g - c * f))
-            py = y + shift[1] + (head * f + (c * e - a * g))
-            pz = z + shift[2] + (head * g + (a * f - b * e))
-            scale = 1.0 / jnp.maximum(-pz, 1.0)
-            u, v = px * scale, py * scale
-            q = u * u + v * v
-            factor = focal * (1.0 + q * (k1 + k2 * q))
-            at_u = pl.ds(2 * (row + h), TILES, stride=4)
-            at_v = pl.ds(2 * (row + h) + 1, TILES, stride=4)
-            ru = factor * u - observed[at_u, :]
-            rv = factor * v - observed[at_v, :]
-            residual[at_u, :] = ru
-            residual[at_v, :] = rv
-            square = ru * ru + rv * rv
-            total = square if total is None else total + square
-        return total
-
-    def turn(i, carry):
-        for u in range(SPREAD):
-            carry = carry + group(i * SPREAD + u, scratch[u])
-        return carry
-
-    cost[...] += lax.fori_loop(
-        0, obs_cam.shape[0] // (2 * TILES * SPREAD), turn, jnp.zeros((8, LANES), jnp.float32)
-    )
-
-
 def camera_rows(trial):
     w = trial[0:3]
     angle = jnp.sqrt(jnp.sum(w * w, axis=0, keepdims=True))
@@ -257,11 +194,21 @@
         copy.wait()
 
 
-def solve_kernel(
-    n_cam, planes, points, gradient, inverse, out,
-    landed, own_points, own_gradient, own_inverse, work, in_sem, send_sum, recv_sum, send_out, recv_out,
+def finish_kernel(
+    n_pts, n_cam, tile_block, tile_points, planes, cam_table, points, gradient, inverse, hbm_cam, hbm_point,
+    hbm_seen, residual, out, sums, landed, own_points, own_gradient, own_inverse, work, obs_cam, obs_point,
+    observed, cam_store, point_table, partial, cam_slots, pts_slots, in_sem, send_sum, recv_sum, send_out,
+    recv_out, send_cam, recv_cam, send_pts, recv_pts, *buffers,
 ):
-    c = lax.axis_index("cam")
+    p, c = lax.axis_index("pts"), lax.axis_index("cam")
+    streams = [
+        pltpu.make_async_copy(source, target, in_sem.at[3 + i])
+        for i, (source, target) in enumerate(
+            ((hbm_cam, obs_cam), (hbm_point, obs_point), (hbm_seen, observed))
+        )
+    ]
+    for stream in streams:
+        stream.start()
     last = n_cam - 1
     chunks = landed.shape[1]
     rows = planes.shape[1] // 2
@@ -284,20 +231,33 @@
         for load in loads:
             load.start()
 
-    barrier = pltpu.get_barrier_semaphore()
+    greet("pts", n_pts, p)
+    greet("cam", n_cam, c)
+
+    def take_cameras(i, carry):
+        for u in range(SPREAD):
+            block = i * SPREAD + u
+            row = pl.multiple_of(block * 2 * TILES, 2 * TILES)
+            buf = buffers[u]
+            for t in range(TILES):
+                slab = cam_table[tile_block[block * TILES + t]]
+                buf[pl.ds(t, 8, stride=PITCH), :] = slab[0:8]
+                buf[pl.ds(8 * PITCH + t, 2, stride=PITCH), :] = slab[8:10]
+            sources = [buf[PITCH * m : PITCH * m + 8, :] for m in range(10)]
+            for h in range(2):
+                index = obs_cam[pl.ds(row + h, TILES, stride=2), :]
+                for m in range(10):
+                    cam_store[m, pl.ds(row + TILES * h, TILES), :] = lane_take(sources[m], index)
+        return carry
+
+    turns = obs_cam.shape[0] // (2 * TILES * SPREAD)
+    early = turns // 4
+    streams[0].wait()
+    lax.fori_loop(0, early, take_cameras, 0)
+    pl.semaphore_wait(pltpu.get_barrier_semaphore(), n_pts + n_cam - 2)
 
     def peer(step):
         return lax.rem(c + step + n_cam, n_cam)
-
-    @pl.when(c > 0)
-    def _():
-        pl.semaphore_signal(barrier, inc=1, device_id={"cam": peer(-1)}, device_id_type=MESH)
-
-    @pl.when(c < last)
-    def _():
-        pl.semaphore_signal(barrier, inc=1, device_id={"cam": peer(1)}, device_id_type=MESH)
-
-    pl.semaphore_wait(barrier, jnp.where(at_end, 1, 2))
 
     def place(way, k):
         base = rows if way == 0 else 0
@@ -336,6 +296,8 @@
                 return carry
 
             lax.fori_loop(0, chunks, begin, 0)
+
+    lax.fori_loop(early, turns, take_cameras, 0)
 
     @pl.when(at_end)
     def _():
@@ -414,16 +376,54 @@
         return carry
 
     lax.fori_loop(0, chunks, finish, 0)
-
-
-def total_kernel(n_pts, n_cam, own, out, cam_slots, pts_slots, send_cam, recv_cam, send_pts, recv_pts):
-    p, c = lax.axis_index("pts"), lax.axis_index("cam")
-    greet("pts", n_pts, p)
-    greet("cam", n_cam, c)
-    cam_slots[c] = own[...]
-    pl.semaphore_wait(pltpu.get_barrier_semaphore(), n_pts + n_cam - 2)
+    for n in range(3):
+        point_table[pl.ds(n, out.shape[1], stride=4), :] = out[n]
+    point_table[pl.ds(3, out.shape[1], stride=4), :] = jnp.zeros_like(out[0])
+    point_slabs = point_table.reshape(point_table.shape[0] // 8, 8, LANES)
+    for stream in streams[1:]:
+        stream.wait()
+
+    def project(i, carry):
+        for u in range(SPREAD):
+            block = i * SPREAD + u
+            row = pl.multiple_of(block * 2 * TILES, 2 * TILES)
+            buf = buffers[u]
+            for t in range(TILES):
+                buf[pl.ds(t, 8, stride=PITCH), :] = point_slabs[tile_points[block * TILES + t]]
+            sources = [buf[PITCH * m : PITCH * m + 8, :] for m in range(8)]
+            for h in range(2):
+                point = obs_point[pl.ds(row + h, TILES, stride=2), :]
+                local = point & (LANES - 1)
+                upper = point >= LANES
+                x, y, z = (
+                    jnp.where(upper, lane_take(sources[4 + n], local), lane_take(sources[n], local))
+                    for n in range(3)
+                )
+                head, a, b, c, *shift, focal, k1, k2 = (
+                    cam_store[m, pl.ds(row + TILES * h, TILES), :] for m in range(10)
+                )
+                e, f, g = b * z - c * y, c * x - a * z, a * y - b * x
+                px = x + shift[0] + (head * e + (b * g - c * f))
+                py = y + shift[1] + (head * f + (c * e - a * g))
+                pz = z + shift[2] + (head * g + (a * f - b * e))
+                scale = 1.0 / jnp.maximum(-pz, 1.0)
+                fu, fv = px * scale, py * scale
+                q = fu * fu + fv * fv
+                factor = focal * (1.0 + q * (k1 + k2 * q))
+                at_u = pl.ds(2 * (row + h), TILES, stride=4)
+                at_v = pl.ds(2 * (row + h) + 1, TILES, stride=4)
+                ru = factor * fu - observed[at_u, :]
+                rv = factor * fv - observed[at_v, :]
+                residual[at_u, :] = ru
+                residual[at_v, :] = rv
+                carry = carry + (ru * ru + rv * rv)
+        return carry
+
+    partial[...] = lax.fori_loop(0, turns, project, jnp.zeros((8, LANES), jnp.float32))
     slot = cam_slots.at[c]
-    for copy in send_round("cam", n_cam, c, lambda *_: own, lambda *_: slot, send_cam, recv_cam):
+    exchange = send_round("cam", n_cam, c, lambda *_: partial, lambda *_: slot, send_cam, recv_cam)
+    cam_slots[c] = partial[...]
+    for copy in exchange:
         copy.wait()
     value = cam_slots[0]
     for i in range(1, n_cam):
@@ -435,7 +435,7 @@
     value = pts_slots[0]
     for i in range(1, n_pts):
         value = value + pts_slots[i]
-    out[...] = value
+    sums[...] = value
 
 
 def on_device(
@@ -513,66 +513,44 @@
 
     own_rows = point_blocks
     chunks = math.gcd(own_rows // 8, CHUNKS)
-    hbm = pl.BlockSpec(memory_space=pl.ANY)
-    trial = pl.pallas_call(
-        functools.partial(solve_kernel, n_cam),
-        in_specs=[vmem, hbm, hbm, hbm],
-        out_specs=vmem,
-        out_shape=jax.ShapeDtypeStruct(planes.shape, jnp.float32),
+    anywhere = pl.BlockSpec(memory_space=pl.ANY)
+    smem = pl.BlockSpec(memory_space=pltpu.SMEM)
+    seen = observed.reshape(2, rows, LANES).transpose(1, 0, 2).reshape(2 * rows, LANES)
+    residual, trial, sums = pl.pallas_call(
+        functools.partial(finish_kernel, n_pts, n_cam),
+        in_specs=[smem, smem, vmem, vmem] + [anywhere] * 6,
+        out_specs=[vmem, vmem, vmem],
+        out_shape=[
+            jax.ShapeDtypeStruct((2 * rows, LANES), jnp.float32),
+            jax.ShapeDtypeStruct(planes.shape, jnp.float32),
+            jax.ShapeDtypeStruct((8, LANES), jnp.float32),
+        ],
         scratch_shapes=[
             pltpu.VMEM((2, chunks, 3, own_rows // chunks, LANES), jnp.float32),
             pltpu.VMEM((3, own_rows * LANES), jnp.float32),
             pltpu.VMEM((3, own_rows * LANES), jnp.float32),
             pltpu.VMEM((9, own_rows * LANES), jnp.float32),
             pltpu.VMEM((15 * (own_rows + 1), LANES), jnp.float32),
-            pltpu.SemaphoreType.DMA((3,)),
-        ]
-        + [pltpu.SemaphoreType.DMA((2, chunks))] * 4,
-        compiler_params=remote(1),
-        name="solve",
-    )(planes, points, point_gradient, point_inverse)
-
-    seen = observed.reshape(2, rows, LANES).transpose(1, 0, 2).reshape(2 * rows, LANES)
-    residual, partial = pl.pallas_call(
-        project_kernel,
-        grid_spec=pltpu.PrefetchScalarGridSpec(
-            num_scalar_prefetch=2,
-            grid=grid,
-            in_specs=[
-                pl.BlockSpec((per, LANES), lambda i, *_: (i, 0)),
-                pl.BlockSpec((per, LANES), lambda i, *_: (i, 0)),
-                pl.BlockSpec((2 * per, LANES), lambda i, *_: (i, 0)),
-                whole(cam_blocks, 16, CB),
-                whole(3, 2 * point_blocks, LANES),
-            ],
-            out_specs=[
-                pl.BlockSpec((2 * per, LANES), lambda i, *_: (i, 0)),
-                whole(8, LANES),
-            ],
-            scratch_shapes=[pltpu.VMEM((point_blocks * 8, LANES), jnp.float32)]
-            + [pltpu.VMEM((18 * PITCH, LANES), jnp.float32)] * SPREAD,
-        ),
-        out_shape=[
-            jax.ShapeDtypeStruct((2 * rows, LANES), jnp.float32),
-            jax.ShapeDtypeStruct((8, LANES), jnp.float32),
-        ],
-        compiler_params=params,
-        name="project",
-    )(tile_block, tile_points, oc, op, seen, cam_table, trial)
-    residual = residual.reshape(rows, 2, LANES).transpose(1, 0, 2).reshape(2, obs_count)
-    sums = pl.pallas_call(
-        functools.partial(total_kernel, n_pts, n_cam),
-        in_specs=[vmem],
-        out_specs=vmem,
-        out_shape=jax.ShapeDtypeStruct((8, LANES), jnp.float32),
-        scratch_shapes=[
+            pltpu.VMEM((rows, LANES), jnp.int32),
+            pltpu.VMEM((rows, LANES), jnp.int32),
+            pltpu.VMEM((2 * rows, LANES), jnp.float32),
+            pltpu.VMEM((10, rows, LANES), jnp.float32),
+            pltpu.VMEM((point_blocks * 8, LANES), jnp.float32),
+            pltpu.VMEM((8, LANES), jnp.float32),
             pltpu.VMEM((n_cam, 8, LANES), jnp.float32),
             pltpu.VMEM((n_pts, 8, LANES), jnp.float32),
+            pltpu.SemaphoreType.DMA((6,)),
         ]
-        + dma_sems(n_cam - 1, n_cam - 1, n_pts - 1, n_pts - 1),
-        compiler_params=remote(2),
-        name="total",
-    )(partial)
+        + [pltpu.SemaphoreType.DMA((2, chunks))] * 4
+        + dma_sems(n_cam - 1, n_cam - 1, n_pts - 1, n_pts - 1)
+        + [pltpu.VMEM((10 * PITCH, LANES), jnp.float32)] * SPREAD,
+        compiler_params=remote(1),
+        name="finish",
+    )(
+        tile_block, tile_points, planes, cam_table, points, point_gradient,
+        point_inverse, oc, op, seen,
+    )
+    residual = residual.reshape(rows, 2, LANES).transpose(1, 0, 2).reshape(2, obs_count)
     trial_cost = jnp.sum(sums) / (2.0 * obs_count * n_pts * n_cam)
     odd = jnp.remainder(accept, 2)
     accepted_points = jnp.where(odd == 1, trial.reshape(3, -1), points)

time: 98.4 us -> 93.4 us (0.949)
  Pallas kernels: 85.6 us -> 79.4 us
  local copies, waits for them, and re-layouts: 4.69 us -> 6 us
    pallas_call x3 -> x1, Pallas kernels: 50.7 us -> 44.4 us  [on_device(): pl.pallas_call(functools.partial(finish_kernel, n_pts, n_cam), in_specs=[...]
    unnamed x16 -> x15, local copies, waits for them, and re-layouts: 3.84 us -> 5.15 us
where the time goes in v4:
time: 93.4 us; the launch traced here: 92.9 us
  Pallas kernels  79.4 us (85%)
  local copies, waits for them, and re-layouts  6 us (6%)
  other arithmetic  4.38 us (5%)
  between operations  3.19 us (3%)
    pallas_call x1, Pallas kernels, on_device(): pl.pallas_call(functools.partial(finish_kernel, n_pts, n_cam), in_specs=[...  44.4 us
    pallas_call x1, Pallas kernels, on_device(): pl.pallas_call(couple_kernel, grid_spec=pltpu.PrefetchScalarGridSpec(num_...  21.1 us
    pallas_call x1, Pallas kernels, on_device(): pl.pallas_call(functools.partial(gather_kernel, n_pts, n_cam), in_specs=[...  13.9 us
    unnamed x15, local copies, waits for them, and re-layouts  5.15 us

profile of v4, /device:TPU:0, one launch (start us, length us, event | category | flops | bytes accessed | tf_op | source)
XLA Modules:
  0.0 92.9 jit_solution(13043986889443592904)
XLA Ops:
  1.3 1.3 %multiply_add_fusion = (f32[9,128]{1,0:T(8,128)}, f32[9,128]{1,0:T(8,128)S(1)}) fusion(f32[9,128]{1,0:T(8,128)} %param.13, f32[9,128]{1,0:T(8,128)} %param.14, f32[]{:T(128)S(6)} %convert_element_type.8), kind=kLoop, calls=%fused_computation.2 | loop fusion | flops 3456 | bytes 18436 | tf_op jit(solution)/shard_map/add | solution.py:557
  2.7 0.8 concatenate.9
  3.5 13.9 %cameras.1 = f32[32,24,128]{2,1,0:T(8,128)S(1)} custom-call(f32[1,24,128]{2,1,0:T(8,128)S(1)} %bitcast.23), custom_call_target="tpu_custom_call" | custom-call | tf_op jit(solution)/shard_map/cameras/pallas_call | solution.py:461
  17.4 0.7 slice_select_fusion.table
  18.2 0.0 copy-start
  18.2 1.2 %copy-done = s32[262144]{0:T(1024)S(1)} copy-done((s32[262144]{0:T(1024)S(1)}, s32[262144]{0:T(1024)}, u32[]{:S(2)}) %copy-start) | copy-done | bytes 1048600
  19.4 0.0 copy-start.1
  19.4 1.2 %copy-done.1 = s32[262144]{0:T(1024)S(1)} copy-done((s32[262144]{0:T(1024)S(1)}, s32[262144]{0:T(1024)}, u32[]{:S(2)}) %copy-start.1) | copy-done | bytes 1048600
  20.7 0.0 copy-start.4
  20.7 0.7 copy-done.4
  21.3 0.0 copy-start.5
  21.3 0.7 copy-done.5
  22.0 0.0 copy-start.2
  22.0 0.0 copy-start.3
  22.0 21.1 %couple.1.planes = f32[3,512,128]{2,1,0:T(8,128)S(1)} custom-call(s32[1024]{0:T(1024)S(1)} %copy-done.4, s32[1024]{0:T(1024)S(1)} %copy-done.5, bf16[18,262144]{1,0:T(8,128)(2,1)} %cam_jac.1, bf16[6,262144]{1,0:T(8,128)(2,1)} %point_jac.1, s32[2048,128]{1,0:T(8,128)S(1)} %bitcast.19, s32[2048,128]{1,0:T(8,128)S(1)} %bitcast.21, ...), custom_call_target="tpu_custom_call" | custom-call | tf_op jit(solution)/shard_map/couple/pallas_call | solution.py:487
  43.1 0.0 copy-done.2
  43.1 0.0 copy-done.3
  43.2 44.4 %finish.1 = (f32[4096,128]{1,0:T(8,128)}, f32[3,512,128]{2,1,0:T(8,128)S(1)}, f32[8,128]{1,0:T(8,128)S(1)}) custom-call(s32[1024]{0:T(1024)S(1)} %copy-done.4, s32[1024]{0:T(1024)S(1)} %copy-done.5, f32[3,512,128]{2,1,0:T(8,128)S(1)} %couple.1.planes, f32[32,16,128]{2,1,0:T(8,128)S(1)} %concatenate.11.cam_table, f32[3,65536]{1,0:T(4,128)S(1)} %copy-done.2, ...), custom_call_target="tpu_custom_call" | custom-call | tf_op jit(solution)/shard_map/finish/pallas_call | solution.py:519
  87.6 0.6 reduce_sum.19
  88.8 0.0 copy-start.6
  88.8 1.6 %bitcast_select_fusion = f32[3,65536]{1,0:T(4,128)} fusion(f32[3,65536]{1,0:T(4,128)S(1)} %copy-done.2, f32[1,3,512,128]{3,2,1,0:T(8,128)S(1)} %bitcast.22, pred[]{:T(512)S(6)} %eq.40), kind=kLoop, calls=%fused_computation | loop fusion | flops 196608 | bytes 2359297 | tf_op jit(solution)/shard_map/jit(_where)/select_n | solution.py:556
  90.5 0.0 copy-done.6
  90.5 1.3 %copy.23 = f32[2,262144]{1,0:T(2,128)} copy(f32[2,262144]{1,0:T(2,128)S(1)} %bitcast.25) | data formatting | bytes 4194304
  (7 shorter events, 0.1 us)
Async XLA Ops:
  18.2 1.2 %copy-start = (s32[262144]{0:T(1024)S(1)}, s32[262144]{0:T(1024)}, u32[]{:S(2)}) copy-start(s32[262144]{0:T(1024)} %param.23) | copy-start | bytes 3145732
  19.4 1.2 %copy-start.1 = (s32[262144]{0:T(1024)S(1)}, s32[262144]{0:T(1024)}, u32[]{:S(2)}) copy-start(s32[262144]{0:T(1024)} %param.24) | copy-start | bytes 3145732
  20.7 0.7 copy-start.4
  21.3 0.7 copy-start.5
  22.0 21.1 %copy-start.2 = (f32[3,65536]{1,0:T(4,128)S(1)}, f32[3,65536]{1,0:T(4,128)}, u32[]{:S(2)}) copy-start(f32[3,65536]{1,0:T(4,128)} %points.1) | copy-start | bytes 2359300
  22.0 21.1 %copy-start.3 = (f32[3,65536]{1,0:T(4,128)S(1)}, f32[3,65536]{1,0:T(4,128)}, u32[]{:S(2)}) copy-start(f32[3,65536]{1,0:T(4,128)} %gradient.1) | copy-start | bytes 2359300
  88.8 1.7 %copy-start.6 = (f32[4096,128]{1,0:T(8,128)S(1)}, f32[4096,128]{1,0:T(8,128)}, u32[]{:S(2)}) copy-start(f32[4096,128]{1,0:T(8,128)} %get-tuple-element.7) | copy-start | bytes 6291460

commit v5 on v4

--- a/solution.py
+++ b/solution.py
@@ -127,8 +127,8 @@
         top = lax.broadcasted_iota(jnp.int32, (8, LANES), 0) < 4
 
         def fold(i, carry):
-            for u in range(8):
-                k = i * 8 + u
+            for u in range(32):
+                k = i * 32 + u
                 base = pl.multiple_of(k * COARSE_ROWS, COARSE_ROWS)
                 parts = [total[pl.ds(base + 8 * j, 8), :] for j in range(4)]
                 pair = [jnp.concatenate(parts[2 * j : 2 * j + 2], axis=1) for j in range(2)]
@@ -136,16 +136,18 @@
                 packed[pl.ds(pl.multiple_of(k * 8, 8), 8), :] = jnp.where(top, *pair)
             return carry
 
-        lax.fori_loop(0, blocks // 8, fold, 0)
+        lax.fori_loop(0, blocks // 32, fold, 0)
         for n in range(3):
             out[n] = packed[pl.ds(n, out.shape[1], stride=4), :]
 
 
 def camera_rows(trial):
     w = trial[0:3]
-    angle = jnp.sqrt(jnp.sum(w * w, axis=0, keepdims=True))
+    angle = jnp.sqrt(w[0:1] * w[0:1] + w[1:2] * w[1:2] + w[2:3] * w[2:3])
     head = math.sqrt(2.0) * jnp.cos(0.5 * angle)
-    tail = math.sqrt(0.5) * jnp.sinc(angle / (2.0 * math.pi)) * w
+    still = angle == 0.0
+    ratio = jnp.where(still, 0.5, jnp.sin(0.5 * angle) / jnp.where(still, 1.0, angle))
+    tail = math.sqrt(2.0) * ratio * w
     return jnp.concatenate([head, tail, trial[3:9]], axis=0)
 
 
@@ -176,28 +178,52 @@
     return copies
 
 
-def gather_kernel(n_pts, n_cam, own, out, local_sem, send_cam, recv_cam, send_pts, recv_pts):
+def gather_kernel(
+    n_pts, n_cam, hbm_cameras, hbm_increment, out, cameras, increment, in_sem, send_cam, recv_cam, send_pts, recv_pts
+):
     p, c = lax.axis_index("pts"), lax.axis_index("cam")
+    loads = [
+        pltpu.make_async_copy(source, target, in_sem.at[i])
+        for i, (source, target) in enumerate(((hbm_cameras, cameras), (hbm_increment, increment)))
+    ]
+    for load in loads:
+        load.start()
     greet("pts", n_pts, p)
     greet("cam", n_cam, c)
+    count = cameras.shape[1] // CB
+    base = (p * n_cam + c) * count
+    for load in loads:
+        load.wait()
+    for i in range(count):
+        lanes = slice(i * CB, (i + 1) * CB)
+        move = increment[:, lanes]
+        trial = cameras[:, lanes] + move
+        out[base + i, 0:9, :] = move
+        out[base + i, 9:19, :] = camera_rows(trial)
     pl.semaphore_wait(pltpu.get_barrier_semaphore(), n_pts + n_cam - 2)
-    count = own.shape[0]
-    mine = out.at[pl.ds((p * n_cam + c) * count, count)]
-    local = pltpu.make_async_copy(own, mine, local_sem)
-    local.start()
-    copies = send_round("cam", n_cam, c, lambda *_: own, lambda *_: mine, send_cam, recv_cam)
-    local.wait()
+
+    def blocks(j):
+        owner = p * n_cam + lax.rem(c - j + n_cam, n_cam)
+        return out.at[pl.ds(owner * count, count), 0:19]
+
+    def forward(j):
+        return send_round("pts", n_pts, p, lambda *_: blocks(j), lambda *_: blocks(j), send_pts.at[j], recv_pts.at[j])
+
+    copies = send_round("cam", n_cam, c, lambda *_: blocks(0), lambda *_: blocks(0), send_cam, recv_cam)
+    forwarded = forward(0)
+    for j in sorted(range(1, n_cam), key=lambda j: min(j, n_cam - j)):
+        copies[j - 1].wait_recv()
+        forwarded += forward(j)
     for copy in copies:
-        copy.wait()
-    slab = out.at[pl.ds(p * n_cam * count, n_cam * count)]
-    for copy in send_round("pts", n_pts, p, lambda *_: slab, lambda *_: slab, send_pts, recv_pts):
+        copy.wait_send()
+    for copy in forwarded:
         copy.wait()
 
 
 def finish_kernel(
     n_pts, n_cam, tile_block, tile_points, planes, cam_table, points, gradient, inverse, hbm_cam, hbm_point,
-    hbm_seen, residual, out, sums, landed, own_points, own_gradient, own_inverse, work, obs_cam, obs_point,
-    observed, cam_store, point_table, partial, cam_slots, pts_slots, in_sem, send_sum, recv_sum, send_out,
+    hbm_seen, residual, point_table, sums, out, landed, own_points, own_gradient, own_inverse, work, obs_cam, obs_point,
+    observed, cam_store, partial, cam_slots, pts_slots, in_sem, send_sum, recv_sum, send_out,
     recv_out, send_cam, recv_cam, send_pts, recv_pts, *buffers,
 ):
     p, c = lax.axis_index("pts"), lax.axis_index("cam")
@@ -438,38 +464,57 @@
     sums[...] = value
 
 
+def emit_kernel(
+    scale, accept, sums, seen, table, points, cameras, increment, residual, cost, accepted_points, accepted_cameras, sem
+):
+    copy = pltpu.make_async_copy(seen, residual, sem)
+    copy.start()
+    odd = (accept[0] & 1) == 1
+    accepted_cameras[...] = cameras[...] + odd.astype(jnp.float32) * increment[...]
+    total = jnp.sum(sums[...], axis=1, keepdims=True)
+    cost[0] = jnp.sum(total) * scale
+
+    def turn(i, carry):
+        for u in range(16):
+            k = i * 16 + u
+            lanes = pl.ds(pl.multiple_of(k * LANES, LANES), LANES)
+            accepted_points[:, lanes] = jnp.where(odd, table[pl.ds(4 * k, 3), :], points[:, lanes])
+        return carry
+
+    lax.fori_loop(0, table.shape[0] // 64, turn, 0)
+    copy.wait()
+
+
 def on_device(
     cameras, increment, points, point_gradient, point_inverse, cam_jacobian, point_jacobian,
     observed, tile_block, tile_points, obs_camera, obs_point, accept,
 ):
     own_blocks = cameras.shape[1] // CB
-    own = jnp.concatenate(
-        [increment, camera_rows(cameras + increment), jnp.zeros((5, cameras.shape[1]), jnp.float32)], axis=0
-    )
-    own = own.reshape(24, own_blocks, CB).transpose(1, 0, 2)
     n_pts, n_cam = lax.axis_size("pts"), lax.axis_size("cam")
     vmem = pl.BlockSpec(memory_space=pltpu.VMEM)
+    hbm = pl.BlockSpec(memory_space=pltpu.HBM)
 
     def dma_sems(*counts):
         return [pltpu.SemaphoreType.DMA((count,)) for count in counts]
 
     def remote(ident):
         return pltpu.CompilerParams(
-            collective_id=ident, has_side_effects=True, vmem_limit_bytes=50 * 2**20
+            collective_id=ident, has_side_effects=True, vmem_limit_bytes=36 * 2**20
         )
 
     every = pl.pallas_call(
         functools.partial(gather_kernel, n_pts, n_cam),
-        in_specs=[vmem],
+        in_specs=[hbm, hbm],
         out_specs=vmem,
         out_shape=jax.ShapeDtypeStruct((own_blocks * n_pts * n_cam, 24, CB), jnp.float32),
-        scratch_shapes=[pltpu.SemaphoreType.DMA]
-        + dma_sems(n_cam - 1, n_cam - 1, n_pts - 1, n_pts - 1),
+        scratch_shapes=[pltpu.VMEM(cameras.shape, jnp.float32)] * 2
+        + dma_sems(2, n_cam - 1, n_cam - 1)
+        + [pltpu.SemaphoreType.DMA((n_cam, n_pts - 1))] * 2,
         compiler_params=remote(0),
+        cost_estimate=pl.CostEstimate(flops=2**30, bytes_accessed=2**20, transcendentals=0),
         name="cameras",
-    )(own)
+    )(cameras, increment)
     cam_blocks = every.shape[0]
-    step_table = jnp.concatenate([every[:, 0:9], jnp.zeros((cam_blocks, 7, CB), jnp.float32)], axis=1)
     cam_table = jnp.concatenate([every[:, 9:19], jnp.zeros((cam_blocks, 6, CB), jnp.float32)], axis=1)
 
     obs_count = obs_camera.shape[0]
@@ -494,7 +539,7 @@
                 pl.BlockSpec((6, per * LANES), lambda i, *_: (0, i)),
                 pl.BlockSpec((per, LANES), lambda i, *_: (i, 0)),
                 pl.BlockSpec((per, LANES), lambda i, *_: (i, 0)),
-                whole(cam_blocks, 16, CB),
+                whole(cam_blocks, 24, CB),
             ],
             out_specs=whole(3, 2 * point_blocks, LANES),
             scratch_shapes=[
@@ -509,23 +554,24 @@
         out_shape=jax.ShapeDtypeStruct((3, 2 * point_blocks, LANES), jnp.float32),
         compiler_params=params,
         name="couple",
-    )(tile_block, tile_points, cam_jacobian, point_jacobian, oc, op, step_table)
+    )(tile_block, tile_points, cam_jacobian, point_jacobian, oc, op, every)
 
     own_rows = point_blocks
     chunks = math.gcd(own_rows // 8, CHUNKS)
     anywhere = pl.BlockSpec(memory_space=pl.ANY)
     smem = pl.BlockSpec(memory_space=pltpu.SMEM)
     seen = observed.reshape(2, rows, LANES).transpose(1, 0, 2).reshape(2 * rows, LANES)
-    residual, trial, sums = pl.pallas_call(
+    residual, point_table, sums = pl.pallas_call(
         functools.partial(finish_kernel, n_pts, n_cam),
         in_specs=[smem, smem, vmem, vmem] + [anywhere] * 6,
         out_specs=[vmem, vmem, vmem],
         out_shape=[
             jax.ShapeDtypeStruct((2 * rows, LANES), jnp.float32),
-            jax.ShapeDtypeStruct(planes.shape, jnp.float32),
+            jax.ShapeDtypeStruct((point_blocks * 8, LANES), jnp.float32),
             jax.ShapeDtypeStruct((8, LANES), jnp.float32),
         ],
         scratch_shapes=[
+            pltpu.VMEM(planes.shape, jnp.float32),
             pltpu.VMEM((2, chunks, 3, own_rows // chunks, LANES), jnp.float32),
             pltpu.VMEM((3, own_rows * LANES), jnp.float32),
             pltpu.VMEM((3, own_rows * LANES), jnp.float32),
@@ -535,7 +581,6 @@
             pltpu.VMEM((rows, LANES), jnp.int32),
             pltpu.VMEM((2 * rows, LANES), jnp.float32),
             pltpu.VMEM((10, rows, LANES), jnp.float32),
-            pltpu.VMEM((point_blocks * 8, LANES), jnp.float32),
             pltpu.VMEM((8, LANES), jnp.float32),
             pltpu.VMEM((n_cam, 8, LANES), jnp.float32),
             pltpu.VMEM((n_pts, 8, LANES), jnp.float32),
@@ -550,11 +595,22 @@
         tile_block, tile_points, planes, cam_table, points, point_gradient,
         point_inverse, oc, op, seen,
     )
+    residual, cost, accepted_points, accepted_cameras = pl.pallas_call(
+        functools.partial(emit_kernel, 1.0 / (2.0 * obs_count * n_pts * n_cam)),
+        in_specs=[smem] + [vmem] * 6,
+        out_specs=[anywhere, smem, vmem, vmem],
+        out_shape=[
+            jax.ShapeDtypeStruct((2 * rows, LANES), jnp.float32),
+            jax.ShapeDtypeStruct((1,), jnp.float32),
+            jax.ShapeDtypeStruct(points.shape, jnp.float32),
+            jax.ShapeDtypeStruct(cameras.shape, jnp.float32),
+        ],
+        scratch_shapes=[pltpu.SemaphoreType.DMA],
+        compiler_params=pltpu.CompilerParams(vmem_limit_bytes=16 * 2**20),
+        name="emit",
+    )(accept.reshape(1), sums, residual, point_table, points, cameras, increment)
     residual = residual.reshape(rows, 2, LANES).transpose(1, 0, 2).reshape(2, obs_count)
-    trial_cost = jnp.sum(sums) / (2.0 * obs_count * n_pts * n_cam)
-    odd = jnp.remainder(accept, 2)
-    accepted_points = jnp.where(odd == 1, trial.reshape(3, -1), points)
-    return residual, trial_cost, accepted_points, cameras + odd.astype(jnp.float32) * increment
+    return residual, cost.reshape(()), accepted_points, accepted_cameras
 
 
 def solution(mesh):

time: 93.4 us -> 81.7 us (0.87)
  local copies, waits for them, and re-layouts: 6 us -> 1.49 us
  other arithmetic: 4.38 us -> 0 us
  between operations: 3.19 us -> 1.63 us
  Pallas kernels: 79.4 us -> 78.3 us
    unnamed x15 -> x24, local copies, waits for them, and re-layouts: 5.15 us -> 1.44 us
    pallas_call x0 -> x1, Pallas kernels: none -> 2.31 us  [on_device(): pl.pallas_call(functools.partial(emit_kernel, 1.0 / (2.0 * obs_count * n_...]
    pallas_call x1, Pallas kernels: 44.4 us -> 42.7 us  [on_device(): pl.pallas_call(functools.partial(finish_kernel, n_pts, n_cam), in_specs=[...]
    select_n x1 -> x0, other arithmetic: 1.64 us -> none  [on_device(): accepted_points = jnp.where(odd == 1, trial.reshape(3, -1), points)]
    add x1 -> x0, other arithmetic: 1.32 us -> none  [on_device(): cameras + odd.astype(jnp.float32) * increment]
where the time goes in v5:
time: 81.7 us; the launch traced here: 81.5 us
  Pallas kernels  78.3 us (96%)
  between operations  1.63 us (2%)
  local copies, waits for them, and re-layouts  1.49 us (2%)
    pallas_call x1, Pallas kernels, on_device(): pl.pallas_call(functools.partial(finish_kernel, n_pts, n_cam), in_specs=[...  42.7 us
    pallas_call x1, Pallas kernels, on_device(): pl.pallas_call(couple_kernel, grid_spec=pltpu.PrefetchScalarGridSpec(num_...  20.3 us
    pallas_call x1, Pallas kernels, on_device(): pl.pallas_call(functools.partial(gather_kernel, n_pts, n_cam), in_specs=[...  13 us
    pallas_call x1, Pallas kernels, on_device(): pl.pallas_call(functools.partial(emit_kernel, 1.0 / (2.0 * obs_count * n_...  2.31 us

profile of v5, /device:TPU:0, one launch (start us, length us, event | category | flops | bytes accessed | tf_op | source)
XLA Modules:
  0.0 81.5 jit_solution(4215855285887672633)
XLA Ops:
  0.6 0.0 copy-start.7
  0.6 0.0 copy-start.6
  0.7 0.0 copy-start.1
  0.7 0.0 copy-start
  1.5 0.0 copy-start.8
  1.5 0.7 copy-done.8
  2.2 0.7 copy-done.10
  2.9 13.0 %cameras.2.table = f32[32,24,128]{2,1,0:T(8,128)S(1)} custom-call(f32[9,128]{1,0:T(8,128)S(1)} %copy-done.8, f32[9,128]{1,0:T(8,128)S(1)} %copy-done.10), custom_call_target="tpu_custom_call" | custom-call | flops 1073741824 | bytes 1048576 | tf_op jit(solution)/shard_map/cameras/pallas_call | solution.py:505
  15.9 0.0 copy-done.7
  15.9 0.0 copy-done.6
  15.9 0.0 copy-done.1
  16.0 0.0 copy-start.2
  16.0 0.0 copy-start.3
  16.0 0.0 copy-start.4
  16.0 0.0 copy-start.5
  16.0 20.3 %couple.1.planes = f32[3,512,128]{2,1,0:T(8,128)S(1)} custom-call(s32[1024]{0:T(1024)S(1)} %copy-done.6, s32[1024]{0:T(1024)S(1)} %copy-done.7, bf16[18,262144]{1,0:T(8,128)(2,1)} %cam_jac.1, bf16[6,262144]{1,0:T(8,128)(2,1)} %point_jac.1, s32[2048,128]{1,0:T(8,128)S(1)} %bitcast.15, s32[2048,128]{1,0:T(8,128)S(1)} %bitcast.17, f32[32,24,128]{2,1,0:T(8,128)S(1)} %cameras.2.table), custom_call_target="tpu_custom_call" | custom-call | tf_op jit(solution)/shard_map/couple/pallas_call | solution.py:532
  36.3 0.0 copy-done.2
  36.3 0.0 copy-done.3
  36.3 0.0 copy-done.4
  36.3 0.0 copy-done.5
  36.4 0.0 copy-start.9
  36.4 0.0 copy-start.11
  36.4 42.7 %finish.1 = (f32[4096,128]{1,0:T(8,128)S(1)}, f32[2048,128]{1,0:T(8,128)S(1)}, f32[8,128]{1,0:T(8,128)S(1)}) custom-call(s32[1024]{0:T(1024)S(1)} %copy-done.6, s32[1024]{0:T(1024)S(1)} %copy-done.7, f32[3,512,128]{2,1,0:T(8,128)S(1)} %couple.1.planes, f32[32,16,128]{2,1,0:T(8,128)S(1)} %concatenate.3.cam_table, f32[3,65536]{1,0:T(4,128)S(1)} %copy-done.2, ...), custom_call_target="tpu_custom_call" | custom-call | tf_op jit(solution)/shard_map/finish/pallas_call | solution.py:564
  79.1 2.3 %emit.1 = (f32[4096,128]{1,0:T(8,128)}, f32[1]{0:T(128)}, f32[3,65536]{1,0:T(4,128)}, f32[9,128]{1,0:T(8,128)}) custom-call(s32[1]{0:T(128)} %bitcast.14.accept, f32[8,128]{1,0:T(8,128)S(1)} %get-tuple-element.11.sums, f32[4096,128]{1,0:T(8,128)S(1)} %get-tuple-element.12.seen, f32[2048,128]{1,0:T(8,128)S(1)} %get-tuple-element.13.table, ...), custom_call_target="tpu_custom_call" | custom-call | tf_op jit(solution)/shard_map/emit/pallas_call | solution.py:598
  (6 shorter events, 0.1 us)
Async XLA Ops:
  0.6 15.3 %copy-start.7 = (s32[1024]{0:T(1024)S(1)}, s32[1024]{0:T(1024)}, u32[]{:S(2)}) copy-start(s32[1024]{0:T(1024)} %tile_points.3) | copy-start | bytes 12292
  0.6 15.3 %copy-start.6 = (s32[1024]{0:T(1024)S(1)}, s32[1024]{0:T(1024)}, u32[]{:S(2)}) copy-start(s32[1024]{0:T(1024)} %tile_block.3) | copy-start | bytes 12292
  0.7 15.3 %copy-start.1 = (s32[262144]{0:T(1024)S(1)}, s32[262144]{0:T(1024)}, u32[]{:S(2)}) copy-start(s32[262144]{0:T(1024)} %param.24) | copy-start | bytes 3145732
  0.7 15.3 %copy-start = (s32[262144]{0:T(1024)S(1)}, s32[262144]{0:T(1024)}, u32[]{:S(2)}) copy-start(s32[262144]{0:T(1024)} %param.23) | copy-start | bytes 3145732
  1.5 0.7 copy-start.8
  2.2 0.7 copy-start.10
  16.0 20.3 %copy-start.2 = (f32[3,65536]{1,0:T(4,128)S(1)}, f32[3,65536]{1,0:T(4,128)}, u32[]{:S(2)}) copy-start(f32[3,65536]{1,0:T(4,128)} %points.3) | copy-start | bytes 2359300
  16.0 20.3 %copy-start.3 = (f32[9,65536]{1,0:T(8,128)S(1)}, f32[9,65536]{1,0:T(8,128)}, u32[]{:S(2)}) copy-start(f32[9,65536]{1,0:T(8,128)} %inverse.1) | copy-start | bytes 7077892
  16.0 20.3 %copy-start.4 = (f32[2,262144]{1,0:T(2,128)S(1)}, f32[2,262144]{1,0:T(2,128)}, u32[]{:S(2)}) copy-start(f32[2,262144]{1,0:T(2,128)} %param.20) | copy-start | bytes 6291460
  16.0 20.3 %copy-start.5 = (f32[3,65536]{1,0:T(4,128)S(1)}, f32[3,65536]{1,0:T(4,128)}, u32[]{:S(2)}) copy-start(f32[3,65536]{1,0:T(4,128)} %gradient.1) | copy-start | bytes 2359300
  36.4 42.8 %copy-start.9 = (f32[9,128]{1,0:T(8,128)S(1)}, f32[9,128]{1,0:T(8,128)}, u32[]{:S(2)}) copy-start(f32[9,128]{1,0:T(8,128)} %cameras.3) | copy-start | bytes 13828
  36.4 42.8 %copy-start.11 = (f32[9,128]{1,0:T(8,128)S(1)}, f32[9,128]{1,0:T(8,128)}, u32[]{:S(2)}) copy-start(f32[9,128]{1,0:T(8,128)} %increment.1) | copy-start | bytes 13828

commit v6 on v5

--- a/solution.py
+++ b/solution.py
@@ -18,7 +18,7 @@
 COARSE_ROWS = 32
 PAIRS = 8
 TILES = 8
-SPREAD = 8
+SPREAD = 16
 CHUNKS = 16
 LAG = 5
 BLOCKS_PER_STEP = 256
@@ -137,8 +137,10 @@
             return carry
 
         lax.fori_loop(0, blocks // 32, fold, 0)
-        for n in range(3):
-            out[n] = packed[pl.ds(n, out.shape[1], stride=4), :]
+        count = out.shape[2]
+        for i in range(out.shape[0]):
+            for n in range(3):
+                out[i, n] = packed[pl.ds(4 * count * i + n, count, stride=4), :]
 
 
 def camera_rows(trial):
@@ -223,8 +225,8 @@
 def finish_kernel(
     n_pts, n_cam, tile_block, tile_points, planes, cam_table, points, gradient, inverse, hbm_cam, hbm_point,
     hbm_seen, residual, point_table, sums, out, landed, own_points, own_gradient, own_inverse, work, obs_cam, obs_point,
-    observed, cam_store, partial, cam_slots, pts_slots, in_sem, send_sum, recv_sum, send_out,
-    recv_out, send_cam, recv_cam, send_pts, recv_pts, *buffers,
+    observed, cam_store, slots, in_sem, send_sum, recv_sum, send_out,
+    recv_out, send_cost, recv_cost, *buffers,
 ):
     p, c = lax.axis_index("pts"), lax.axis_index("cam")
     streams = [
@@ -237,8 +239,8 @@
         stream.start()
     last = n_cam - 1
     chunks = landed.shape[1]
-    rows = planes.shape[1] // 2
-    count = rows // chunks
+    count = planes.shape[2]
+    rows = count * chunks
     span, pitch = rows * LANES, rows + 1
     low_end, high_end = c == 0, c == last
     at_end = jnp.logical_or(low_end, high_end)
@@ -258,7 +260,18 @@
             load.start()
 
     greet("pts", n_pts, p)
-    greet("cam", n_cam, c)
+    barrier = pltpu.get_barrier_semaphore()
+
+    def peer(step):
+        return lax.rem(c + step + n_cam, n_cam)
+
+    @pl.when(c > 0)
+    def _():
+        pl.semaphore_signal(barrier, inc=1, device_id={"cam": peer(-1)}, device_id_type=MESH)
+
+    @pl.when(c < last)
+    def _():
+        pl.semaphore_signal(barrier, inc=1, device_id={"cam": peer(1)}, device_id_type=MESH)
 
     def take_cameras(i, carry):
         for u in range(SPREAD):
@@ -280,14 +293,10 @@
     early = turns // 4
     streams[0].wait()
     lax.fori_loop(0, early, take_cameras, 0)
-    pl.semaphore_wait(pltpu.get_barrier_semaphore(), n_pts + n_cam - 2)
-
-    def peer(step):
-        return lax.rem(c + step + n_cam, n_cam)
+    pl.semaphore_wait(barrier, n_pts - 1 + jnp.where(at_end, 1, 2))
 
     def place(way, k):
-        base = rows if way == 0 else 0
-        return pl.ds(pl.multiple_of(base + k * count, 8), count)
+        return k + chunks if way == 0 else k
 
     def toward(way):
         return peer(1) if way == 0 else peer(-1)
@@ -303,7 +312,7 @@
         )
 
     def out_copy(way, k):
-        part = out.at[:, place(way, k)]
+        part = out.at[place(way, k)]
         return pltpu.make_async_remote_copy(
             src_ref=part,
             dst_ref=part,
@@ -318,7 +327,7 @@
         @pl.when(first)
         def _(way=way):
             def begin(k, carry):
-                sum_copy(way, k, planes.at[:, place(way, k)]).start()
+                sum_copy(way, k, planes.at[place(way, k)]).start()
                 return carry
 
             lax.fori_loop(0, chunks, begin, 0)
@@ -347,11 +356,11 @@
         def row(m):
             return work[pl.ds(m * pitch + k * count, count), :]
 
-        total = landed[way, k] + planes[:, place(way, k), :]
+        total = landed[way, k] + planes[place(way, k)]
         residue = [row(3 + n) - total[n] for n in range(3)]
         for n in range(3):
             move = row(6 + 3 * n) * residue[0] + row(7 + 3 * n) * residue[1] + row(8 + 3 * n) * residue[2]
-            out[n, place(way, k), :] = row(n) + move
+            out[place(way, k), n] = row(n) + move
 
     def turn(s, carry):
         for way, hops in ((0, c), (1, last - c)):
@@ -364,7 +373,7 @@
 
                 @pl.when(hops < last)
                 def _():
-                    landed[way, k] = landed[way, k] + planes[:, place(way, k), :]
+                    landed[way, k] = landed[way, k] + planes[place(way, k)]
                     sum_copy(way, k, landed.at[way, k]).start()
 
                 @pl.when(hops == last)
@@ -402,9 +411,10 @@
         return carry
 
     lax.fori_loop(0, chunks, finish, 0)
-    for n in range(3):
-        point_table[pl.ds(n, out.shape[1], stride=4), :] = out[n]
-    point_table[pl.ds(3, out.shape[1], stride=4), :] = jnp.zeros_like(out[0])
+    point_table[...] = jnp.zeros_like(point_table)
+    for i in range(2 * chunks):
+        for n in range(3):
+            point_table[pl.ds(4 * count * i + n, count, stride=4), :] = out[i, n]
     point_slabs = point_table.reshape(point_table.shape[0] // 8, 8, LANES)
     for stream in streams[1:]:
         stream.wait()
@@ -445,23 +455,28 @@
                 carry = carry + (ru * ru + rv * rv)
         return carry
 
-    partial[...] = lax.fori_loop(0, turns, project, jnp.zeros((8, LANES), jnp.float32))
-    slot = cam_slots.at[c]
-    exchange = send_round("cam", n_cam, c, lambda *_: partial, lambda *_: slot, send_cam, recv_cam)
-    cam_slots[c] = partial[...]
-    for copy in exchange:
+    cost = lax.fori_loop(0, turns, project, jnp.zeros((8, LANES), jnp.float32))
+    me = p * n_cam + c
+    slots[pl.ds(me, 1), :] = jnp.sum(cost, axis=0, keepdims=True)
+    mine = slots.at[pl.ds(me, 1)]
+    copies = []
+    for j in range(1, n_pts * n_cam):
+        step_p, step_c = j // n_cam, j % n_cam
+        copies.append(
+            pltpu.make_async_remote_copy(
+                src_ref=mine,
+                dst_ref=mine,
+                send_sem=send_cost.at[j],
+                recv_sem=recv_cost.at[j],
+                device_id={"pts": lax.rem(p + step_p, n_pts), "cam": lax.rem(c + step_c, n_cam)},
+                device_id_type=MESH,
+            )
+        )
+    for copy in copies:
+        copy.start()
+    for copy in copies:
         copy.wait()
-    value = cam_slots[0]
-    for i in range(1, n_cam):
-        value = value + cam_slots[i]
-    pts_slots[p] = value
-    slot = pts_slots.at[p]
-    for copy in send_round("pts", n_pts, p, lambda *_: slot, lambda *_: slot, send_pts, recv_pts):
-        copy.wait()
-    value = pts_slots[0]
-    for i in range(1, n_pts):
-        value = value + pts_slots[i]
-    sums[...] = value
+    sums[...] = jnp.sum(slots[...], axis=0, keepdims=True)
 
 
 def emit_kernel(
@@ -471,8 +486,7 @@
     copy.start()
     odd = (accept[0] & 1) == 1
     accepted_cameras[...] = cameras[...] + odd.astype(jnp.float32) * increment[...]
-    total = jnp.sum(sums[...], axis=1, keepdims=True)
-    cost[0] = jnp.sum(total) * scale
+    cost[0] = jnp.sum(sums[...]) * scale
 
     def turn(i, carry):
         for u in range(16):
@@ -522,6 +536,7 @@
     per = math.gcd(rows, BLOCKS_PER_STEP)
     grid = (rows // per,)
     point_blocks = points.shape[1] // PB
+    chunks = math.gcd(point_blocks // 8, CHUNKS)
     oc = obs_camera.reshape(rows, LANES)
     op = obs_point.reshape(rows, LANES)
 
@@ -541,7 +556,7 @@
                 pl.BlockSpec((per, LANES), lambda i, *_: (i, 0)),
                 whole(cam_blocks, 24, CB),
             ],
-            out_specs=whole(3, 2 * point_blocks, LANES),
+            out_specs=whole(2 * chunks, 3, point_blocks // chunks, LANES),
             scratch_shapes=[
                 pltpu.VMEM((point_blocks * COARSE_ROWS, FINE), jnp.float32),
                 pltpu.VMEM((point_blocks * 8, LANES), jnp.float32),
@@ -551,13 +566,12 @@
             ]
             * PAIRS,
         ),
-        out_shape=jax.ShapeDtypeStruct((3, 2 * point_blocks, LANES), jnp.float32),
+        out_shape=jax.ShapeDtypeStruct((2 * chunks, 3, point_blocks // chunks, LANES), jnp.float32),
         compiler_params=params,
         name="couple",
     )(tile_block, tile_points, cam_jacobian, point_jacobian, oc, op, every)
 
     own_rows = point_blocks
-    chunks = math.gcd(own_rows // 8, CHUNKS)
     anywhere = pl.BlockSpec(memory_space=pl.ANY)
     smem = pl.BlockSpec(memory_space=pltpu.SMEM)
     seen = observed.reshape(2, rows, LANES).transpose(1, 0, 2).reshape(2 * rows, LANES)
@@ -568,7 +582,7 @@
         out_shape=[
             jax.ShapeDtypeStruct((2 * rows, LANES), jnp.float32),
             jax.ShapeDtypeStruct((point_blocks * 8, LANES), jnp.float32),
-            jax.ShapeDtypeStruct((8, LANES), jnp.float32),
+            jax.ShapeDtypeStruct((1, LANES), jnp.float32),
         ],
         scratch_shapes=[
             pltpu.VMEM(planes.shape, jnp.float32),
@@ -581,13 +595,11 @@
             pltpu.VMEM((rows, LANES), jnp.int32),
             pltpu.VMEM((2 * rows, LANES), jnp.float32),
             pltpu.VMEM((10, rows, LANES), jnp.float32),
-            pltpu.VMEM((8, LANES), jnp.float32),
-            pltpu.VMEM((n_cam, 8, LANES), jnp.float32),
-            pltpu.VMEM((n_pts, 8, LANES), jnp.float32),
+            pltpu.VMEM((n_pts * n_cam, LANES), jnp.float32),
             pltpu.SemaphoreType.DMA((6,)),
         ]
         + [pltpu.SemaphoreType.DMA((2, chunks))] * 4
-        + dma_sems(n_cam - 1, n_cam - 1, n_pts - 1, n_pts - 1)
+        + dma_sems(n_pts * n_cam, n_pts * n_cam)
         + [pltpu.VMEM((10 * PITCH, LANES), jnp.float32)] * SPREAD,
         compiler_params=remote(1),
         name="finish",

time: 81.7 us -> 78.8 us (0.965)
  Pallas kernels: 78.3 us -> 75.4 us
    pallas_call x1, Pallas kernels: 42.7 us -> 39.8 us  [on_device(): pl.pallas_call(functools.partial(finish_kernel, n_pts, n_cam), in_specs=[...]
where the time goes in v6:
time: 78.8 us; the launch traced here: 78.5 us
  Pallas kernels  75.4 us (96%)
  between operations  1.63 us (2%)
  local copies, waits for them, and re-layouts  1.49 us (2%)
    pallas_call x1, Pallas kernels, on_device(): pl.pallas_call(functools.partial(finish_kernel, n_pts, n_cam), in_specs=[...  39.8 us
    pallas_call x1, Pallas kernels, on_device(): pl.pallas_call(couple_kernel, grid_spec=pltpu.PrefetchScalarGridSpec(num_...  20.3 us
    pallas_call x1, Pallas kernels, on_device(): pl.pallas_call(functools.partial(gather_kernel, n_pts, n_cam), in_specs=[...  13 us
    pallas_call x1, Pallas kernels, on_device(): pl.pallas_call(functools.partial(emit_kernel, 1.0 / (2.0 * obs_count * n_...  2.31 us

profile of v6, /device:TPU:0, one launch (start us, length us, event | category | flops | bytes accessed | tf_op | source)
XLA Modules:
  0.0 78.5 jit_solution(15557817825323684829)
XLA Ops:
  0.6 0.0 copy-start.7
  0.6 0.0 copy-start.6
  0.7 0.0 copy-start.1
  0.7 0.0 copy-start
  1.5 0.0 copy-start.8
  1.5 0.7 copy-done.8
  2.2 0.7 copy-done.10
  2.9 13.0 %cameras.2.table = f32[32,24,128]{2,1,0:T(8,128)S(1)} custom-call(f32[9,128]{1,0:T(8,128)S(1)} %copy-done.8, f32[9,128]{1,0:T(8,128)S(1)} %copy-done.10), custom_call_target="tpu_custom_call" | custom-call | flops 1073741824 | bytes 1048576 | tf_op jit(solution)/shard_map/cameras/pallas_call | solution.py:519
  15.9 0.0 copy-done.7
  15.9 0.0 copy-done.6
  15.9 0.0 copy-done.1
  16.0 0.0 copy-done
  16.0 0.0 copy-start.2
  16.0 0.0 copy-start.3
  16.0 0.0 copy-start.4
  16.0 0.0 copy-start.5
  16.0 20.3 %couple.1.planes = f32[32,3,16,128]{3,2,1,0:T(8,128)S(1)} custom-call(s32[1024]{0:T(1024)S(1)} %copy-done.6, s32[1024]{0:T(1024)S(1)} %copy-done.7, bf16[18,262144]{1,0:T(8,128)(2,1)} %cam_jac.1, bf16[6,262144]{1,0:T(8,128)(2,1)} %point_jac.1, s32[2048,128]{1,0:T(8,128)S(1)} %bitcast.15, s32[2048,128]{1,0:T(8,128)S(1)} %bitcast.17, ...), custom_call_target="tpu_custom_call" | custom-call | tf_op jit(solution)/shard_map/couple/pallas_call | solution.py:547
  36.3 0.0 copy-done.2
  36.3 0.0 copy-done.3
  36.3 0.0 copy-done.4
  36.3 0.0 copy-start.9
  36.3 0.0 copy-start.11
  36.4 39.8 %finish.1 = (f32[4096,128]{1,0:T(8,128)S(1)}, f32[2048,128]{1,0:T(8,128)S(1)}, f32[1,128]{1,0:T(1,128)S(1)}) custom-call(s32[1024]{0:T(1024)S(1)} %copy-done.6, s32[1024]{0:T(1024)S(1)} %copy-done.7, f32[32,3,16,128]{3,2,1,0:T(8,128)S(1)} %couple.1.planes, f32[32,16,128]{2,1,0:T(8,128)S(1)} %concatenate.3.cam_table, f32[3,65536]{1,0:T(4,128)S(1)} %copy-done.2, ...), custom_call_target="tpu_custom_call" | custom-call | tf_op jit(solution)/shard_map/finish/pallas_call | solution.py:578
  76.2 2.3 %emit.1 = (f32[4096,128]{1,0:T(8,128)}, f32[1]{0:T(128)}, f32[3,65536]{1,0:T(4,128)}, f32[9,128]{1,0:T(8,128)}) custom-call(s32[1]{0:T(128)} %bitcast.14.accept, f32[1,128]{1,0:T(1,128)S(1)} %get-tuple-element.11.sums, f32[4096,128]{1,0:T(8,128)S(1)} %get-tuple-element.12.seen, f32[2048,128]{1,0:T(8,128)S(1)} %get-tuple-element.13.table, ...), custom_call_target="tpu_custom_call" | custom-call | tf_op jit(solution)/shard_map/emit/pallas_call | solution.py:610
  (6 shorter events, 0.1 us)
Async XLA Ops:
  0.6 15.3 %copy-start.7 = (s32[1024]{0:T(1024)S(1)}, s32[1024]{0:T(1024)}, u32[]{:S(2)}) copy-start(s32[1024]{0:T(1024)} %tile_points.3) | copy-start | bytes 12292
  0.6 15.3 %copy-start.6 = (s32[1024]{0:T(1024)S(1)}, s32[1024]{0:T(1024)}, u32[]{:S(2)}) copy-start(s32[1024]{0:T(1024)} %tile_block.3) | copy-start | bytes 12292
  0.7 15.3 %copy-start.1 = (s32[262144]{0:T(1024)S(1)}, s32[262144]{0:T(1024)}, u32[]{:S(2)}) copy-start(s32[262144]{0:T(1024)} %param.24) | copy-start | bytes 3145732
  0.7 15.3 %copy-start = (s32[262144]{0:T(1024)S(1)}, s32[262144]{0:T(1024)}, u32[]{:S(2)}) copy-start(s32[262144]{0:T(1024)} %param.23) | copy-start | bytes 3145732
  1.5 0.7 copy-start.8
  2.2 0.7 copy-start.10
  16.0 20.3 %copy-start.2 = (f32[3,65536]{1,0:T(4,128)S(1)}, f32[3,65536]{1,0:T(4,128)}, u32[]{:S(2)}) copy-start(f32[3,65536]{1,0:T(4,128)} %points.3) | copy-start | bytes 2359300
  16.0 20.3 %copy-start.3 = (f32[9,65536]{1,0:T(8,128)S(1)}, f32[9,65536]{1,0:T(8,128)}, u32[]{:S(2)}) copy-start(f32[9,65536]{1,0:T(8,128)} %inverse.1) | copy-start | bytes 7077892
  16.0 20.3 %copy-start.4 = (f32[2,262144]{1,0:T(2,128)S(1)}, f32[2,262144]{1,0:T(2,128)}, u32[]{:S(2)}) copy-start(f32[2,262144]{1,0:T(2,128)} %param.20) | copy-start | bytes 6291460
  16.0 20.3 %copy-start.5 = (f32[3,65536]{1,0:T(4,128)S(1)}, f32[3,65536]{1,0:T(4,128)}, u32[]{:S(2)}) copy-start(f32[3,65536]{1,0:T(4,128)} %gradient.1) | copy-start | bytes 2359300
  36.3 39.8 %copy-start.9 = (f32[9,128]{1,0:T(8,128)S(1)}, f32[9,128]{1,0:T(8,128)}, u32[]{:S(2)}) copy-start(f32[9,128]{1,0:T(8,128)} %cameras.3) | copy-start | bytes 13828
  36.3 39.8 %copy-start.11 = (f32[9,128]{1,0:T(8,128)S(1)}, f32[9,128]{1,0:T(8,128)}, u32[]{:S(2)}) copy-start(f32[9,128]{1,0:T(8,128)} %increment.1) | copy-start | bytes 13828

commit v7 on v6

--- a/solution.py
+++ b/solution.py
@@ -17,8 +17,9 @@
 FINE_BITS = 6
 COARSE_ROWS = 32
 PAIRS = 8
+SPLIT = 2
 TILES = 8
-SPREAD = 16
+SPREAD = 32
 CHUNKS = 16
 LAG = 5
 BLOCKS_PER_STEP = 256
@@ -41,16 +42,18 @@
 
 
 def couple_kernel(
-    tile_block, tile_points, cam_jac, point_jac, obs_cam, obs_point, table, out, total, packed, *scratch
+    tile_block, tile_points, cam_jac, point_jac, obs_cam, obs_point, table, out, packed, *scratch
 ):
     step = pl.program_id(0)
     tiles_per_step = obs_cam.shape[0] // 2
+    totals, scratch = scratch[:SPLIT], scratch[SPLIT:]
     buffers = [scratch[5 * u : 5 * u + 5] for u in range(PAIRS)]
     blocks = packed.shape[0] // 8
 
     @pl.when(step == 0)
     def _():
-        total[...] = jnp.zeros_like(total)
+        for total in totals:
+            total[...] = jnp.zeros_like(total)
         for _, _, _, low, high in buffers:
             low[...] = jnp.zeros_like(low)
             high[...] = jnp.zeros_like(high)
@@ -113,6 +116,7 @@
                 preferred_element_type=jnp.float32,
             )
             place = pl.ds(pl.multiple_of(tile_points[tile + t] * COARSE_ROWS, COARSE_ROWS), COARSE_ROWS)
+            total = totals[t % SPLIT]
             total[place, :] = total[place, :] + summed
 
     def turn(i, carry):
@@ -130,7 +134,7 @@
             for u in range(32):
                 k = i * 32 + u
                 base = pl.multiple_of(k * COARSE_ROWS, COARSE_ROWS)
-                parts = [total[pl.ds(base + 8 * j, 8), :] for j in range(4)]
+                parts = [sum(total[pl.ds(base + 8 * j, 8), :] for total in totals) for j in range(4)]
                 pair = [jnp.concatenate(parts[2 * j : 2 * j + 2], axis=1) for j in range(2)]
                 pair = [value + pltpu.roll(value, 4, 0) for value in pair]
                 packed[pl.ds(pl.multiple_of(k * 8, 8), 8), :] = jnp.where(top, *pair)
@@ -558,9 +562,9 @@
             ],
             out_specs=whole(2 * chunks, 3, point_blocks // chunks, LANES),
             scratch_shapes=[
-                pltpu.VMEM((point_blocks * COARSE_ROWS, FINE), jnp.float32),
                 pltpu.VMEM((point_blocks * 8, LANES), jnp.float32),
             ]
+            + [pltpu.VMEM((point_blocks * COARSE_ROWS, FINE), jnp.float32)] * SPLIT
             + [
                 pltpu.VMEM((count * PITCH, LANES), jnp.float32) for count in (9, 24, 24, 10, 10)
             ]

time: 78.8 us -> 77.6 us (0.985)
  Pallas kernels: 75.4 us -> 74.2 us
    pallas_call x1, Pallas kernels: 20.3 us -> 19.5 us  [on_device(): pl.pallas_call(couple_kernel, grid_spec=pltpu.PrefetchScalarGridSpec(num_...]
where the time goes in v7:
time: 77.6 us; the launch traced here: 77.3 us
  Pallas kernels  74.2 us (96%)
  between operations  1.63 us (2%)
  local copies, waits for them, and re-layouts  1.49 us (2%)
    pallas_call x1, Pallas kernels, on_device(): pl.pallas_call(functools.partial(finish_kernel, n_pts, n_cam), in_specs=[...  39.4 us
    pallas_call x1, Pallas kernels, on_device(): pl.pallas_call(couple_kernel, grid_spec=pltpu.PrefetchScalarGridSpec(num_...  19.5 us
    pallas_call x1, Pallas kernels, on_device(): pl.pallas_call(functools.partial(gather_kernel, n_pts, n_cam), in_specs=[...  13 us
    pallas_call x1, Pallas kernels, on_device(): pl.pallas_call(functools.partial(emit_kernel, 1.0 / (2.0 * obs_count * n_...  2.31 us

profile of v7, /device:TPU:0, one launch (start us, length us, event | category | flops | bytes accessed | tf_op | source)
XLA Modules:
  0.0 77.3 jit_solution(7579350041834150777)
XLA Ops:
  0.6 0.0 copy-start.7
  0.6 0.0 copy-start.6
  0.7 0.0 copy-start.1
  0.7 0.0 copy-start
  1.5 0.0 copy-start.8
  1.5 0.7 copy-done.8
  2.2 0.7 copy-done.10
  2.9 13.0 %cameras.2.table = f32[32,24,128]{2,1,0:T(8,128)S(1)} custom-call(f32[9,128]{1,0:T(8,128)S(1)} %copy-done.8, f32[9,128]{1,0:T(8,128)S(1)} %copy-done.10), custom_call_target="tpu_custom_call" | custom-call | flops 1073741824 | bytes 1048576 | tf_op jit(solution)/shard_map/cameras/pallas_call | solution.py:523
  15.9 0.0 copy-done.7
  15.9 0.0 copy-done.6
  15.9 0.0 copy-done.1
  16.0 0.0 copy-start.2
  16.0 0.0 copy-start.3
  16.0 0.0 copy-start.4
  16.0 0.0 copy-start.5
  16.0 19.5 %couple.1.planes = f32[32,3,16,128]{3,2,1,0:T(8,128)S(1)} custom-call(s32[1024]{0:T(1024)S(1)} %copy-done.6, s32[1024]{0:T(1024)S(1)} %copy-done.7, bf16[18,262144]{1,0:T(8,128)(2,1)} %cam_jac.1, bf16[6,262144]{1,0:T(8,128)(2,1)} %point_jac.1, s32[2048,128]{1,0:T(8,128)S(1)} %bitcast.15, s32[2048,128]{1,0:T(8,128)S(1)} %bitcast.17, ...), custom_call_target="tpu_custom_call" | custom-call | tf_op jit(solution)/shard_map/couple/pallas_call | solution.py:551
  35.5 0.0 copy-done.2
  35.5 0.0 copy-done.3
  35.5 0.0 copy-done.4
  35.5 0.0 copy-done.5
  35.5 0.0 copy-start.9
  35.6 0.0 copy-start.11
  35.6 39.4 %finish.1 = (f32[4096,128]{1,0:T(8,128)S(1)}, f32[2048,128]{1,0:T(8,128)S(1)}, f32[1,128]{1,0:T(1,128)S(1)}) custom-call(s32[1024]{0:T(1024)S(1)} %copy-done.6, s32[1024]{0:T(1024)S(1)} %copy-done.7, f32[32,3,16,128]{3,2,1,0:T(8,128)S(1)} %couple.1.planes, f32[32,16,128]{2,1,0:T(8,128)S(1)} %concatenate.3.cam_table, f32[3,65536]{1,0:T(4,128)S(1)} %copy-done.2, ...), custom_call_target="tpu_custom_call" | custom-call | tf_op jit(solution)/shard_map/finish/pallas_call | solution.py:582
  75.0 2.3 %emit.1 = (f32[4096,128]{1,0:T(8,128)}, f32[1]{0:T(128)}, f32[3,65536]{1,0:T(4,128)}, f32[9,128]{1,0:T(8,128)}) custom-call(s32[1]{0:T(128)} %bitcast.14.accept, f32[1,128]{1,0:T(1,128)S(1)} %get-tuple-element.11.sums, f32[4096,128]{1,0:T(8,128)S(1)} %get-tuple-element.12.seen, f32[2048,128]{1,0:T(8,128)S(1)} %get-tuple-element.13.table, ...), custom_call_target="tpu_custom_call" | custom-call | tf_op jit(solution)/shard_map/emit/pallas_call | solution.py:614
  (6 shorter events, 0.1 us)
Async XLA Ops:
  0.6 15.3 %copy-start.7 = (s32[1024]{0:T(1024)S(1)}, s32[1024]{0:T(1024)}, u32[]{:S(2)}) copy-start(s32[1024]{0:T(1024)} %tile_points.3) | copy-start | bytes 12292
  0.6 15.3 %copy-start.6 = (s32[1024]{0:T(1024)S(1)}, s32[1024]{0:T(1024)}, u32[]{:S(2)}) copy-start(s32[1024]{0:T(1024)} %tile_block.3) | copy-start | bytes 12292
  0.7 15.3 %copy-start.1 = (s32[262144]{0:T(1024)S(1)}, s32[262144]{0:T(1024)}, u32[]{:S(2)}) copy-start(s32[262144]{0:T(1024)} %param.24) | copy-start | bytes 3145732
  0.7 15.3 %copy-start = (s32[262144]{0:T(1024)S(1)}, s32[262144]{0:T(1024)}, u32[]{:S(2)}) copy-start(s32[262144]{0:T(1024)} %param.23) | copy-start | bytes 3145732
  1.5 0.7 copy-start.8
  2.2 0.7 copy-start.10
  16.0 19.5 %copy-start.2 = (f32[3,65536]{1,0:T(4,128)S(1)}, f32[3,65536]{1,0:T(4,128)}, u32[]{:S(2)}) copy-start(f32[3,65536]{1,0:T(4,128)} %points.3) | copy-start | bytes 2359300
  16.0 19.5 %copy-start.3 = (f32[9,65536]{1,0:T(8,128)S(1)}, f32[9,65536]{1,0:T(8,128)}, u32[]{:S(2)}) copy-start(f32[9,65536]{1,0:T(8,128)} %inverse.1) | copy-start | bytes 7077892
  16.0 19.5 %copy-start.4 = (f32[2,262144]{1,0:T(2,128)S(1)}, f32[2,262144]{1,0:T(2,128)}, u32[]{:S(2)}) copy-start(f32[2,262144]{1,0:T(2,128)} %param.20) | copy-start | bytes 6291460
  16.0 19.5 %copy-start.5 = (f32[3,65536]{1,0:T(4,128)S(1)}, f32[3,65536]{1,0:T(4,128)}, u32[]{:S(2)}) copy-start(f32[3,65536]{1,0:T(4,128)} %gradient.1) | copy-start | bytes 2359300
  35.5 39.5 %copy-start.9 = (f32[9,128]{1,0:T(8,128)S(1)}, f32[9,128]{1,0:T(8,128)}, u32[]{:S(2)}) copy-start(f32[9,128]{1,0:T(8,128)} %cameras.3) | copy-start | bytes 13828
  35.6 39.5 %copy-start.11 = (f32[9,128]{1,0:T(8,128)S(1)}, f32[9,128]{1,0:T(8,128)}, u32[]{:S(2)}) copy-start(f32[9,128]{1,0:T(8,128)} %increment.1) | copy-start | bytes 13828

commit v8 on v7

--- a/solution.py
+++ b/solution.py
@@ -16,7 +16,7 @@
 FINE = 64
 FINE_BITS = 6
 COARSE_ROWS = 32
-PAIRS = 8
+PAIRS = 16
 SPLIT = 2
 TILES = 8
 SPREAD = 32
@@ -184,26 +184,16 @@
     return copies
 
 
-def gather_kernel(
-    n_pts, n_cam, hbm_cameras, hbm_increment, out, cameras, increment, in_sem, send_cam, recv_cam, send_pts, recv_pts
-):
+def gather_kernel(n_pts, n_cam, own, out, send_cam, recv_cam, send_pts, recv_pts):
     p, c = lax.axis_index("pts"), lax.axis_index("cam")
-    loads = [
-        pltpu.make_async_copy(source, target, in_sem.at[i])
-        for i, (source, target) in enumerate(((hbm_cameras, cameras), (hbm_increment, increment)))
-    ]
-    for load in loads:
-        load.start()
     greet("pts", n_pts, p)
     greet("cam", n_cam, c)
-    count = cameras.shape[1] // CB
+    count = own.shape[2] // CB
     base = (p * n_cam + c) * count
-    for load in loads:
-        load.wait()
     for i in range(count):
         lanes = slice(i * CB, (i + 1) * CB)
-        move = increment[:, lanes]
-        trial = cameras[:, lanes] + move
+        move = own[1, :, lanes]
+        trial = own[0, :, lanes] + move
         out[base + i, 0:9, :] = move
         out[base + i, 9:19, :] = camera_rows(trial)
     pl.semaphore_wait(pltpu.get_barrier_semaphore(), n_pts + n_cam - 2)
@@ -522,16 +512,15 @@
 
     every = pl.pallas_call(
         functools.partial(gather_kernel, n_pts, n_cam),
-        in_specs=[hbm, hbm],
+        in_specs=[vmem],
         out_specs=vmem,
         out_shape=jax.ShapeDtypeStruct((own_blocks * n_pts * n_cam, 24, CB), jnp.float32),
-        scratch_shapes=[pltpu.VMEM(cameras.shape, jnp.float32)] * 2
-        + dma_sems(2, n_cam - 1, n_cam - 1)
+        scratch_shapes=dma_sems(n_cam - 1, n_cam - 1)
         + [pltpu.SemaphoreType.DMA((n_cam, n_pts - 1))] * 2,
         compiler_params=remote(0),
         cost_estimate=pl.CostEstimate(flops=2**30, bytes_accessed=2**20, transcendentals=0),
         name="cameras",
-    )(cameras, increment)
+    )(jnp.stack([cameras, increment]))
     cam_blocks = every.shape[0]
     cam_table = jnp.concatenate([every[:, 9:19], jnp.zeros((cam_blocks, 6, CB), jnp.float32)], axis=1)
 

time: 77.6 us -> 73.9 us (0.952)
  Pallas kernels: 74.2 us -> 71.1 us
  local copies, waits for them, and re-layouts: 1.49 us -> 0.1 us
    pallas_call x1, Pallas kernels: 19.5 us -> 16.4 us  [on_device(): pl.pallas_call(couple_kernel, grid_spec=pltpu.PrefetchScalarGridSpec(num_...]
    unnamed x24 -> x20, local copies, waits for them, and re-layouts: 1.44 us -> 0.05 us
where the time goes in v8:
time: 73.9 us; the launch traced here: 73.5 us
  Pallas kernels  71.1 us (96%)
  between operations  1.63 us (2%)
    pallas_call x1, Pallas kernels, on_device(): pl.pallas_call(functools.partial(finish_kernel, n_pts, n_cam), in_specs=[...  39.4 us
    pallas_call x1, Pallas kernels, on_device(): pl.pallas_call(couple_kernel, grid_spec=pltpu.PrefetchScalarGridSpec(num_...  16.4 us
    pallas_call x1, Pallas kernels, on_device(): pl.pallas_call(functools.partial(gather_kernel, n_pts, n_cam), in_specs=[...  13 us
    pallas_call x1, Pallas kernels, on_device(): pl.pallas_call(functools.partial(emit_kernel, 1.0 / (2.0 * obs_count * n_...  2.31 us

profile of v8, /device:TPU:0, one launch (start us, length us, event | category | flops | bytes accessed | tf_op | source)
XLA Modules:
  0.0 73.5 jit_solution(4773189741693250241)
XLA Ops:
  0.6 0.0 copy-start.9
  0.6 0.0 copy-start.8
  0.7 0.0 copy-start.1
  0.7 0.0 copy-start
  1.5 0.7 pad_maximum_fusion.own
  2.2 13.0 %cameras.2.table = f32[32,24,128]{2,1,0:T(8,128)S(1)} custom-call(f32[2,9,128]{2,1,0:T(8,128)S(1)} %pad_maximum_fusion.own), custom_call_target="tpu_custom_call" | custom-call | flops 1073741824 | bytes 1048576 | tf_op jit(solution)/shard_map/cameras/pallas_call | solution.py:513
  15.2 0.0 copy-done.9
  15.2 0.0 copy-done.8
  15.2 0.0 copy-done.1
  15.3 0.0 copy-done
  15.3 0.0 copy-start.2
  15.3 0.0 copy-start.3
  15.3 0.0 copy-start.4
  15.3 0.0 copy-start.5
  15.3 16.4 %couple.1.planes = f32[32,3,16,128]{3,2,1,0:T(8,128)S(1)} custom-call(s32[1024]{0:T(1024)S(1)} %copy-done.8, s32[1024]{0:T(1024)S(1)} %copy-done.9, bf16[18,262144]{1,0:T(8,128)(2,1)} %cam_jac.1, bf16[6,262144]{1,0:T(8,128)(2,1)} %point_jac.1, s32[2048,128]{1,0:T(8,128)S(1)} %bitcast.17, s32[2048,128]{1,0:T(8,128)S(1)} %bitcast.19, ...), custom_call_target="tpu_custom_call" | custom-call | tf_op jit(solution)/shard_map/couple/pallas_call | solution.py:540
  31.7 0.0 copy-done.2
  31.8 0.0 copy-done.3
  31.8 0.0 copy-done.4
  31.8 0.0 copy-done.5
  31.8 0.0 copy-start.6
  31.8 0.0 copy-start.7
  31.8 39.4 %finish.1 = (f32[4096,128]{1,0:T(8,128)S(1)}, f32[2048,128]{1,0:T(8,128)S(1)}, f32[1,128]{1,0:T(1,128)S(1)}) custom-call(s32[1024]{0:T(1024)S(1)} %copy-done.8, s32[1024]{0:T(1024)S(1)} %copy-done.9, f32[32,3,16,128]{3,2,1,0:T(8,128)S(1)} %couple.1.planes, f32[32,16,128]{2,1,0:T(8,128)S(1)} %concatenate.3.cam_table, f32[3,65536]{1,0:T(4,128)S(1)} %copy-done.2, ...), custom_call_target="tpu_custom_call" | custom-call | tf_op jit(solution)/shard_map/finish/pallas_call | solution.py:571
  71.2 0.0 copy-done.6
  71.2 2.3 %emit.1 = (f32[4096,128]{1,0:T(8,128)}, f32[1]{0:T(128)}, f32[3,65536]{1,0:T(4,128)}, f32[9,128]{1,0:T(8,128)}) custom-call(s32[1]{0:T(128)} %bitcast.16.accept, f32[1,128]{1,0:T(1,128)S(1)} %get-tuple-element.11.sums, f32[4096,128]{1,0:T(8,128)S(1)} %get-tuple-element.12.seen, f32[2048,128]{1,0:T(8,128)S(1)} %get-tuple-element.13.table, ...), custom_call_target="tpu_custom_call" | custom-call | tf_op jit(solution)/shard_map/emit/pallas_call | solution.py:603
  (3 shorter events, 0.0 us)
Async XLA Ops:
  0.6 14.6 %copy-start.9 = (s32[1024]{0:T(1024)S(1)}, s32[1024]{0:T(1024)}, u32[]{:S(2)}) copy-start(s32[1024]{0:T(1024)} %tile_points.3) | copy-start | bytes 12292
  0.6 14.6 %copy-start.8 = (s32[1024]{0:T(1024)S(1)}, s32[1024]{0:T(1024)}, u32[]{:S(2)}) copy-start(s32[1024]{0:T(1024)} %tile_block.3) | copy-start | bytes 12292
  0.7 14.6 %copy-start.1 = (s32[262144]{0:T(1024)S(1)}, s32[262144]{0:T(1024)}, u32[]{:S(2)}) copy-start(s32[262144]{0:T(1024)} %param.24) | copy-start | bytes 3145732
  0.7 14.6 %copy-start = (s32[262144]{0:T(1024)S(1)}, s32[262144]{0:T(1024)}, u32[]{:S(2)}) copy-start(s32[262144]{0:T(1024)} %param.23) | copy-start | bytes 3145732
  15.3 16.5 %copy-start.2 = (f32[3,65536]{1,0:T(4,128)S(1)}, f32[3,65536]{1,0:T(4,128)}, u32[]{:S(2)}) copy-start(f32[3,65536]{1,0:T(4,128)} %points.3) | copy-start | bytes 2359300
  15.3 16.5 %copy-start.3 = (f32[9,65536]{1,0:T(8,128)S(1)}, f32[9,65536]{1,0:T(8,128)}, u32[]{:S(2)}) copy-start(f32[9,65536]{1,0:T(8,128)} %inverse.1) | copy-start | bytes 7077892
  15.3 16.5 %copy-start.4 = (f32[2,262144]{1,0:T(2,128)S(1)}, f32[2,262144]{1,0:T(2,128)}, u32[]{:S(2)}) copy-start(f32[2,262144]{1,0:T(2,128)} %param.20) | copy-start | bytes 6291460
  15.3 16.5 %copy-start.5 = (f32[3,65536]{1,0:T(4,128)S(1)}, f32[3,65536]{1,0:T(4,128)}, u32[]{:S(2)}) copy-start(f32[3,65536]{1,0:T(4,128)} %gradient.1) | copy-start | bytes 2359300
  31.8 39.4 %copy-start.6 = (f32[9,128]{1,0:T(8,128)S(1)}, f32[9,128]{1,0:T(8,128)}, u32[]{:S(2)}) copy-start(f32[9,128]{1,0:T(8,128)} %increment.1) | copy-start | bytes 13828
  31.8 39.4 %copy-start.7 = (f32[9,128]{1,0:T(8,128)S(1)}, f32[9,128]{1,0:T(8,128)}, u32[]{:S(2)}) copy-start(f32[9,128]{1,0:T(8,128)} %cameras.3) | copy-start | bytes 13828

commit v9 on v8

--- a/solution.py
+++ b/solution.py
@@ -131,8 +131,8 @@
         top = lax.broadcasted_iota(jnp.int32, (8, LANES), 0) < 4
 
         def fold(i, carry):
-            for u in range(32):
-                k = i * 32 + u
+            for u in range(64):
+                k = i * 64 + u
                 base = pl.multiple_of(k * COARSE_ROWS, COARSE_ROWS)
                 parts = [sum(total[pl.ds(base + 8 * j, 8), :] for total in totals) for j in range(4)]
                 pair = [jnp.concatenate(parts[2 * j : 2 * j + 2], axis=1) for j in range(2)]
@@ -140,7 +140,7 @@
                 packed[pl.ds(pl.multiple_of(k * 8, 8), 8), :] = jnp.where(top, *pair)
             return carry
 
-        lax.fori_loop(0, blocks // 32, fold, 0)
+        lax.fori_loop(0, blocks // 64, fold, 0)
         count = out.shape[2]
         for i in range(out.shape[0]):
             for n in range(3):
@@ -466,7 +466,7 @@
                 device_id_type=MESH,
             )
         )
-    for copy in copies:
+    for copy in reversed(copies):
         copy.start()
     for copy in copies:
         copy.wait()

time: 73.9 us -> 73.7 us (level)
  no operation moved by 1% of the time
where the time goes in v9:
time: 73.7 us; the launch traced here: 73.3 us
  Pallas kernels  70.9 us (96%)
  between operations  1.63 us (2%)
    pallas_call x1, Pallas kernels, on_device(): pl.pallas_call(functools.partial(finish_kernel, n_pts, n_cam), in_specs=[...  39.5 us
    pallas_call x1, Pallas kernels, on_device(): pl.pallas_call(couple_kernel, grid_spec=pltpu.PrefetchScalarGridSpec(num_...  16.1 us
    pallas_call x1, Pallas kernels, on_device(): pl.pallas_call(functools.partial(gather_kernel, n_pts, n_cam), in_specs=[...  13 us
    pallas_call x1, Pallas kernels, on_device(): pl.pallas_call(functools.partial(emit_kernel, 1.0 / (2.0 * obs_count * n_...  2.31 us

profile of v9, /device:TPU:0, one launch (start us, length us, event | category | flops | bytes accessed | tf_op | source)
XLA Modules:
  0.0 73.3 jit_solution(9102308686833935811)
XLA Ops:
  0.6 0.0 copy-start.9
  0.6 0.0 copy-start.8
  0.7 0.0 copy-start.1
  0.7 0.0 copy-start
  1.5 0.7 pad_maximum_fusion.own
  2.2 13.0 %cameras.2.table = f32[32,24,128]{2,1,0:T(8,128)S(1)} custom-call(f32[2,9,128]{2,1,0:T(8,128)S(1)} %pad_maximum_fusion.own), custom_call_target="tpu_custom_call" | custom-call | flops 1073741824 | bytes 1048576 | tf_op jit(solution)/shard_map/cameras/pallas_call | solution.py:513
  15.2 0.0 copy-done.9
  15.2 0.0 copy-done.8
  15.2 0.0 copy-done.1
  15.3 0.0 copy-done
  15.3 0.0 copy-start.2
  15.3 0.0 copy-start.3
  15.3 0.0 copy-start.4
  15.3 0.0 copy-start.5
  15.3 16.1 %couple.1.planes = f32[32,3,16,128]{3,2,1,0:T(8,128)S(1)} custom-call(s32[1024]{0:T(1024)S(1)} %copy-done.8, s32[1024]{0:T(1024)S(1)} %copy-done.9, bf16[18,262144]{1,0:T(8,128)(2,1)} %cam_jac.1, bf16[6,262144]{1,0:T(8,128)(2,1)} %point_jac.1, s32[2048,128]{1,0:T(8,128)S(1)} %bitcast.17, s32[2048,128]{1,0:T(8,128)S(1)} %bitcast.19, ...), custom_call_target="tpu_custom_call" | custom-call | tf_op jit(solution)/shard_map/couple/pallas_call | solution.py:540
  31.5 0.0 copy-done.2
  31.5 0.0 copy-done.3
  31.5 0.0 copy-done.4
  31.5 0.0 copy-done.5
  31.5 0.0 copy-start.6
  31.5 0.0 copy-start.7
  31.5 39.5 %finish.1 = (f32[4096,128]{1,0:T(8,128)S(1)}, f32[2048,128]{1,0:T(8,128)S(1)}, f32[1,128]{1,0:T(1,128)S(1)}) custom-call(s32[1024]{0:T(1024)S(1)} %copy-done.8, s32[1024]{0:T(1024)S(1)} %copy-done.9, f32[32,3,16,128]{3,2,1,0:T(8,128)S(1)} %couple.1.planes, f32[32,16,128]{2,1,0:T(8,128)S(1)} %concatenate.3.cam_table, f32[3,65536]{1,0:T(4,128)S(1)} %copy-done.2, ...), custom_call_target="tpu_custom_call" | custom-call | tf_op jit(solution)/shard_map/finish/pallas_call | solution.py:571
  71.0 0.0 copy-done.6
  71.0 2.3 %emit.1 = (f32[4096,128]{1,0:T(8,128)}, f32[1]{0:T(128)}, f32[3,65536]{1,0:T(4,128)}, f32[9,128]{1,0:T(8,128)}) custom-call(s32[1]{0:T(128)} %bitcast.16.accept, f32[1,128]{1,0:T(1,128)S(1)} %get-tuple-element.11.sums, f32[4096,128]{1,0:T(8,128)S(1)} %get-tuple-element.12.seen, f32[2048,128]{1,0:T(8,128)S(1)} %get-tuple-element.13.table, ...), custom_call_target="tpu_custom_call" | custom-call | tf_op jit(solution)/shard_map/emit/pallas_call | solution.py:603
  (3 shorter events, 0.0 us)
Async XLA Ops:
  0.6 14.6 %copy-start.9 = (s32[1024]{0:T(1024)S(1)}, s32[1024]{0:T(1024)}, u32[]{:S(2)}) copy-start(s32[1024]{0:T(1024)} %tile_points.3) | copy-start | bytes 12292
  0.6 14.6 %copy-start.8 = (s32[1024]{0:T(1024)S(1)}, s32[1024]{0:T(1024)}, u32[]{:S(2)}) copy-start(s32[1024]{0:T(1024)} %tile_block.3) | copy-start | bytes 12292
  0.7 14.6 %copy-start.1 = (s32[262144]{0:T(1024)S(1)}, s32[262144]{0:T(1024)}, u32[]{:S(2)}) copy-start(s32[262144]{0:T(1024)} %param.24) | copy-start | bytes 3145732
  0.7 14.6 %copy-start = (s32[262144]{0:T(1024)S(1)}, s32[262144]{0:T(1024)}, u32[]{:S(2)}) copy-start(s32[262144]{0:T(1024)} %param.23) | copy-start | bytes 3145732
  15.3 16.2 %copy-start.2 = (f32[3,65536]{1,0:T(4,128)S(1)}, f32[3,65536]{1,0:T(4,128)}, u32[]{:S(2)}) copy-start(f32[3,65536]{1,0:T(4,128)} %points.3) | copy-start | bytes 2359300
  15.3 16.2 %copy-start.3 = (f32[9,65536]{1,0:T(8,128)S(1)}, f32[9,65536]{1,0:T(8,128)}, u32[]{:S(2)}) copy-start(f32[9,65536]{1,0:T(8,128)} %inverse.1) | copy-start | bytes 7077892
  15.3 16.2 %copy-start.4 = (f32[2,262144]{1,0:T(2,128)S(1)}, f32[2,262144]{1,0:T(2,128)}, u32[]{:S(2)}) copy-start(f32[2,262144]{1,0:T(2,128)} %param.20) | copy-start | bytes 6291460
  15.3 16.2 %copy-start.5 = (f32[3,65536]{1,0:T(4,128)S(1)}, f32[3,65536]{1,0:T(4,128)}, u32[]{:S(2)}) copy-start(f32[3,65536]{1,0:T(4,128)} %gradient.1) | copy-start | bytes 2359300
  31.5 39.5 %copy-start.6 = (f32[9,128]{1,0:T(8,128)S(1)}, f32[9,128]{1,0:T(8,128)}, u32[]{:S(2)}) copy-start(f32[9,128]{1,0:T(8,128)} %increment.1) | copy-start | bytes 13828
  31.5 39.5 %copy-start.7 = (f32[9,128]{1,0:T(8,128)S(1)}, f32[9,128]{1,0:T(8,128)}, u32[]{:S(2)}) copy-start(f32[9,128]{1,0:T(8,128)} %cameras.3) | copy-start | bytes 13828
